TPU v7x, 32 devices: a 4x2x2 block of a 4x4x8 slice. The times are simulated.
32 devices in a mesh: dp: 4 (over y, z), tp: 8 (over x, core).
Axes of the slice: x: 4, y: 2, z: 2, core: 2. Of those that a mesh axis runs over, the one named last changes fastest.
The devices are a block of a 4x4x8 slice.
Arguments:
- x: bfloat16 [768, 2048], P('dp'), parts along dimension 0
- lengths: int32 [260], P('dp'), parts along dimension 0
- attn_gain: bfloat16 [2, 2048], replicated
- w_q: bfloat16 [2, 2048, 2048], P(None, None, 'tp')
- w_k: bfloat16 [2, 2048, 512], P(None, None, 'tp')
- w_v: bfloat16 [2, 2048, 512], P(None, None, 'tp')
- w_o: bfloat16 [2, 2048, 2048], P(None, 'tp')
- mlp_gain: bfloat16 [2, 2048], replicated
- w_gate: bfloat16 [2, 2048, 8192], P(None, None, 'tp')
- w_up: bfloat16 [2, 2048, 8192], P(None, None, 'tp')
- w_down: bfloat16 [2, 8192, 2048], P(None, 'tp')
- k_cache: bfloat16 [2, 260, 8, 1024, 64], P(None, 'dp', 'tp'), parts along dimension 1
- v_cache: bfloat16 [2, 260, 8, 1024, 64], P(None, 'dp', 'tp'), parts along dimension 1
Outputs:
- output: bfloat16 [768, 2048], P('dp'), parts along dimension 0
There are 4 independent parts. A program takes and returns all parts, laid end to end along the dimension named above; an argument that names none is the same for every part.
All inputs are finite; a program needn't handle non-finite values.
Results may differ from a plain program's by a relative error of at most 0.02.
Values are sent between devices in bfloat16 or wider.
A program may use at most 768 MiB of HBM per device.

v0:
```python
import jax
import jax.numpy as jnp
from jax import lax
from jax.sharding import PartitionSpec as P

ROPE_BASE = 500000.0
EPSILON = 1e-5


def rms_norm(x, norm_gain):
    x_f32 = x.astype(jnp.float32)
    inv_rms = lax.rsqrt(jnp.mean(x_f32 * x_f32, axis=-1, keepdims=True) + EPSILON)
    return (x_f32 * inv_rms * norm_gain.astype(jnp.float32)).astype(jnp.bfloat16)


def rope_tables(positions, head_dim):
    freq_exps = jnp.arange(0, head_dim, 2, dtype=jnp.float32) / head_dim
    angles = positions.astype(jnp.float32)[:, None] * jnp.power(ROPE_BASE, -freq_exps)[None, :]
    return jnp.cos(angles)[:, None, :], jnp.sin(angles)[:, None, :]


def apply_rope(vectors, cos_tab, sin_tab):
    half_dim = vectors.shape[-1] // 2
    vec_f32 = vectors.astype(jnp.float32)
    first = vec_f32[..., :half_dim]
    second = vec_f32[..., half_dim:]
    return jnp.concatenate([first * cos_tab - second * sin_tab, second * cos_tab + first * sin_tab], axis=-1).astype(jnp.bfloat16)


def project(normed, weight, head_dim):
    return jnp.dot(normed, weight, preferred_element_type=jnp.float32).astype(jnp.bfloat16).reshape(normed.shape[0], -1, head_dim)


def attention(q_rot, k_rot, v_new, k_cache, v_cache, lengths):
    dec_rows = lengths.shape[0] - 1
    kv_local = k_cache.shape[1]
    seq_len = k_cache.shape[2]
    head_dim = k_cache.shape[3]
    tok_count = q_rot.shape[0]
    chunk_len = tok_count - dec_rows
    attn_scale = head_dim ** -0.5
    q_grouped = q_rot.reshape(tok_count, kv_local, -1, head_dim)
    q_dec = q_grouped[:dec_rows]
    q_chk = q_grouped[dec_rows:]
    seq_ids = jnp.arange(seq_len)
    dec_cache = jnp.einsum('bgrd,bgsd->bgrs', q_dec, k_cache[:dec_rows], preferred_element_type=jnp.float32) * attn_scale
    dec_cache = jnp.where(seq_ids[None, None, None, :] < lengths[:dec_rows, None, None, None], dec_cache, -jnp.inf)
    dec_self = jnp.einsum('bgrd,bgd->bgr', q_dec, k_rot[:dec_rows], preferred_element_type=jnp.float32)[..., None] * attn_scale
    dec_prob = jax.nn.softmax(jnp.concatenate([dec_cache, dec_self], axis=-1), axis=-1).astype(jnp.bfloat16)
    dec_out = jnp.einsum('bgrs,bgsd->bgrd', dec_prob[..., :seq_len], v_cache[:dec_rows], preferred_element_type=jnp.float32) + dec_prob[..., seq_len:].astype(jnp.float32) * v_new[:dec_rows, :, None, :].astype(jnp.float32)
    chk_cache = jnp.einsum('cgrd,gsd->cgrs', q_chk, k_cache[dec_rows], preferred_element_type=jnp.float32) * attn_scale
    chk_cache = jnp.where(seq_ids[None, None, None, :] < lengths[dec_rows], chk_cache, -jnp.inf)
    chk_self = jnp.einsum('cgrd,jgd->cgrj', q_chk, k_rot[dec_rows:], preferred_element_type=jnp.float32) * attn_scale
    tok_ids = jnp.arange(chunk_len)
    causal_mask = tok_ids[None, :] <= tok_ids[:, None]
    chk_self = jnp.where(causal_mask[:, None, None, :], chk_self, -jnp.inf)
    chk_prob = jax.nn.softmax(jnp.concatenate([chk_cache, chk_self], axis=-1), axis=-1).astype(jnp.bfloat16)
    chk_out = jnp.einsum('cgrs,gsd->cgrd', chk_prob[..., :seq_len], v_cache[dec_rows], preferred_element_type=jnp.float32) + jnp.einsum('cgrj,jgd->cgrd', chk_prob[..., seq_len:], v_new[dec_rows:], preferred_element_type=jnp.float32)
    return jnp.concatenate([dec_out.reshape(dec_rows, -1), chk_out.reshape(chunk_len, -1)], axis=0).astype(jnp.bfloat16)


def decoder_layer(x, cos_tab, sin_tab, lengths, attn_gain, w_q, w_k, w_v, w_o, mlp_gain, w_gate, w_up, w_down, k_cache, v_cache):
    head_dim = k_cache.shape[-1]
    normed = rms_norm(x, attn_gain)
    q_rot = apply_rope(project(normed, w_q, head_dim), cos_tab, sin_tab)
    k_rot = apply_rope(project(normed, w_k, head_dim), cos_tab, sin_tab)
    v_new = project(normed, w_v, head_dim)
    attended = attention(q_rot, k_rot, v_new, k_cache, v_cache, lengths)
    attn_part = jnp.dot(attended, w_o, preferred_element_type=jnp.float32).astype(jnp.bfloat16)
    attn_sum = lax.psum(attn_part, 'tp')
    hidden = (x.astype(jnp.float32) + attn_sum.astype(jnp.float32)).astype(jnp.bfloat16)
    mlp_in = rms_norm(hidden, mlp_gain)
    gate_proj = jnp.dot(mlp_in, w_gate, preferred_element_type=jnp.float32)
    up_proj = jnp.dot(mlp_in, w_up, preferred_element_type=jnp.float32)
    activated = (jax.nn.silu(gate_proj) * up_proj).astype(jnp.bfloat16)
    mlp_part = jnp.dot(activated, w_down, preferred_element_type=jnp.float32).astype(jnp.bfloat16)
    mlp_sum = lax.psum(mlp_part, 'tp')
    return (hidden.astype(jnp.float32) + mlp_sum.astype(jnp.float32)).astype(jnp.bfloat16)


def solution(mesh):
    col_spec = P(None, None, 'tp')
    row_spec = P(None, 'tp', None)
    cache_spec = P(None, 'dp', 'tp', None, None)
    in_specs = (P('dp', None), P('dp'), P(), col_spec, col_spec, col_spec, row_spec, P(), col_spec, col_spec, row_spec, cache_spec, cache_spec)

    def body(x, lengths, attn_gain, w_q, w_k, w_v, w_o, mlp_gain, w_gate, w_up, w_down, k_cache, v_cache):
        dec_rows = lengths.shape[0] - 1
        chunk_len = x.shape[0] - dec_rows
        positions = jnp.concatenate([lengths[:dec_rows], lengths[dec_rows] + jnp.arange(chunk_len, dtype=jnp.int32)])
        cos_tab, sin_tab = rope_tables(positions, k_cache.shape[-1])
        hidden = x
        for layer_idx in range(w_q.shape[0]):
            hidden = decoder_layer(hidden, cos_tab, sin_tab, lengths, attn_gain[layer_idx], w_q[layer_idx], w_k[layer_idx], w_v[layer_idx], w_o[layer_idx], mlp_gain[layer_idx], w_gate[layer_idx], w_up[layer_idx], w_down[layer_idx], k_cache[layer_idx], v_cache[layer_idx])
        return hidden

    return jax.shard_map(body, mesh=mesh, in_specs=in_specs, out_specs=P('dp', None), check_vma=False)
```

profile of v0, /device:TPU:81, one launch (start us, length us, event | category | flops | bytes accessed | tf_op | source)
XLA Modules:
  0.0 333.1 jit_solution(9147227690138311086)
XLA Ops:
  12.8 1.9 fusion.71
  17.4 4.6 %fusion.3 = f32[64,4,1024]{2,1,0:T(4,128)S(1)} fusion(bf16[192,4,64]{2,1,0:T(4,128)(2,1)S(1)} %pad_maximum_fusion, bf16[2,65,1,1024,64]{3,4,1,2,0:T(8,128)(2,1)} %bitcast.263), kind=kOutput, calls=%fused_computation.7 | convolution fusion | flops 33554432 | bytes 9535488 | tf_op jit(solution)/shard_map/bgrd,bgsd->bgrs/dot_general | solution.py:46
  22.0 2.0 copy.115
  24.0 2.7 fusion.37
  27.0 2.0 fusion.93
  29.0 1.8 divide_convert_fusion.3
  32.8 5.6 %fusion.77 = bf16[64,4,64]{2,1,0:T(4,128)(2,1)S(1)} fusion(bf16[64,4,1024]{2,1,0:T(4,128)(2,1)S(1)} %copy.120, bf16[2,65,1,1024,64]{3,4,1,2,0:T(8,128)(2,1)} %bitcast.267, f32[64,64]{1,0:T(8,128)S(1)} %copy.122, f32[64,4]{1,0:T(8,128)S(1)} %copy.121), kind=kOutput, calls=%fused_computation.103 | convolution fusion | flops 33603584 | bytes 8963072 | tf_op jit(solution)/shard_map/bgrs,bgsd->bgrd/dot_general | solution.py:50
  44.7 57.6 %all-reduce.5.cloned.1.call-done = bf16[192,2048]{1,0:T(8,128)(2,1)} async-done(((bf16[192,2048]{1,0:T(8,128)(2,1)}), bf16[192,2048]{1,0:T(8,128)(2,1)}) %all-reduce.5.cloned.1.call-update) | async-done | bytes 786448 | tf_op jit(solution)/shard_map/psum | solution.py:70
  103.8 3.2 fusion.14
  107.0 6.3 %fusion.22 = bf16[192,2048]{1,0:T(8,128)(2,1)} fusion(bf16[2,1024,2048]{2,1,0:T(8,128)(2,1)} %param.23, bf16[2,2048,1024]{2,1,0:T(8,128)(2,1)} %param.22, f32[192,1024]{1,0:T(8,128)S(1)} %fusion.14, bf16[192,2048]{1,0:T(8,128)(2,1)S(1)} %get-tuple-element.8, f32[2048]{0:T(1024)S(1)} %bitcast.262, f32[192]{0:T(256)S(1)} %add_rsqrt_fusion.2), kind=kOutput, calls=%fused_computation.26 | convolution fusion | flops 1613758464 | bytes 10756864 | tf_op jit(solution)/shard_map/dot_general | solution.py:76
  113.7 54.6 %all-reduce.7.cloned.1.call-done = bf16[192,2048]{1,0:T(8,128)(2,1)} async-done(((bf16[192,2048]{1,0:T(8,128)(2,1)}), bf16[192,2048]{1,0:T(8,128)(2,1)}) %all-reduce.7.cloned.1.call-update) | async-done | bytes 786448 | tf_op jit(solution)/shard_map/psum | solution.py:77
  173.6 4.6 %fusion.1 = f32[64,4,1024]{2,1,0:T(4,128)S(1)} fusion(bf16[192,4,64]{2,1,0:T(4,128)(2,1)S(1)} %pad_maximum_fusion.1, bf16[2,65,1,1024,64]{3,4,1,2,0:T(8,128)(2,1)} %bitcast.264), kind=kOutput, calls=%fused_computation.3 | convolution fusion | flops 33554432 | bytes 9535488 | tf_op jit(solution)/shard_map/bgrd,bgsd->bgrs/dot_general | solution.py:46
  178.4 1.8 copy.131
  180.2 2.7 fusion.39
  183.2 2.0 fusion.92
  185.1 1.8 divide_convert_fusion.2
  190.4 2.6 copy.136
  193.1 5.8 %fusion.76 = bf16[64,4,64]{2,1,0:T(4,128)(2,1)S(1)} fusion(bf16[64,4,1024]{2,1,0:T(4,128)(2,1)} %copy.136, bf16[2,65,1,1024,64]{3,4,1,2,0:T(8,128)(2,1)} %bitcast.268, f32[64,64]{1,0:T(8,128)S(1)} %copy.138, f32[64,4]{1,0:T(8,128)S(1)} %copy.137), kind=kOutput, calls=%fused_computation.102 | convolution fusion | flops 33603584 | bytes 8963072 | tf_op jit(solution)/shard_map/bgrs,bgsd->bgrd/dot_general | solution.py:50
  203.3 54.8 %all-reduce.9.cloned.1.call-done = bf16[192,2048]{1,0:T(8,128)(2,1)} async-done(((bf16[192,2048]{1,0:T(8,128)(2,1)}), bf16[192,2048]{1,0:T(8,128)(2,1)}) %all-reduce.9.cloned.1.call-update) | async-done | bytes 786448 | tf_op jit(solution)/shard_map/psum | solution.py:70
  258.1 1.6 fusion.52
  259.7 3.2 fusion.8
  262.9 6.4 %fusion.25 = bf16[192,2048]{1,0:T(8,128)(2,1)} fusion(bf16[2,1024,2048]{2,1,0:T(8,128)(2,1)} %param.23, bf16[2,2048,1024]{2,1,0:T(8,128)(2,1)} %param.22, f32[192,1024]{1,0:T(8,128)S(1)} %fusion.8, bf16[192,2048]{1,0:T(8,128)(2,1)S(1)} %get-tuple-element.6, f32[2048]{0:T(1024)S(1)} %bitcast.257, f32[192]{0:T(256)S(1)} %add_rsqrt_fusion), kind=kOutput, calls=%fused_computation.27 | convolution fusion | flops 1613758464 | bytes 10756864 | tf_op jit(solution)/shard_map/dot_general | solution.py:76
  269.3 54.9 %all-reduce.11.cloned.1.call-done = bf16[192,2048]{1,0:T(8,128)(2,1)} async-done(((bf16[192,2048]{1,0:T(8,128)(2,1)}), bf16[192,2048]{1,0:T(8,128)(2,1)}) %all-reduce.11.cloned.1.call-update) | async-done | bytes 786448 | tf_op jit(solution)/shard_map/psum | solution.py:77
  324.2 2.3 fusion.55
  (114 shorter events, 32.5 us)
Async XLA Ops:
  6.5 95.8 %all-reduce.5.cloned.1.call-start = ((), (), s32[]{:S(2)}) async-start(), calls=%async_computation | async-start | bytes 1572864 | tf_op jit(solution)/shard_map/psum | solution.py:70
  14.8 1.6 copy-start.2
  14.8 1.6 copy-start.5
  29.0 2.2 copy-start.7
  40.9 2.2 copy-start.3
  41.4 3.2 copy-start.9
  44.6 123.7 %all-reduce.7.cloned.1.call-start = ((), (), s32[]{:S(2)}) async-start(), calls=%async_computation.1 | async-start | bytes 1572864 | tf_op jit(solution)/shard_map/psum | solution.py:77
  113.4 56.8 %copy-start.8 = (bf16[2,2048,64]{1,2,0:T(8,128)(2,1)S(1)}, bf16[2,2048,64]{1,2,0:T(8,128)(2,1)}, u32[]{:S(2)}) copy-start(bf16[2,2048,64]{1,2,0:T(8,128)(2,1)} %param.18) | copy-start | bytes 1572868
  113.4 144.7 %all-reduce.9.cloned.1.call-start = ((), (), s32[]{:S(2)}) async-start(), calls=%async_computation.2 | async-start | bytes 1572864 | tf_op jit(solution)/shard_map/psum | solution.py:70
  168.3 1.6 copy-start
  169.8 1.0 copy-start.6
  169.8 1.7 copy-start.10
  199.5 2.2 copy-start.4
  200.0 58.0 %copy-start.1 = (bf16[192,2048]{1,0:T(8,128)(2,1)S(1)}, bf16[192,2048]{1,0:T(8,128)(2,1)}, u32[]{:S(2)}) copy-start(bf16[192,2048]{1,0:T(8,128)(2,1)} %all-reduce.7.cloned.1.call-done) | copy-start | bytes 2359300
  203.2 121.0 %all-reduce.11.cloned.1.call-start = ((), (), s32[]{:S(2)}) async-start(), calls=%async_computation.3 | async-start | bytes 1572864 | tf_op jit(solution)/shard_map/psum | solution.py:77
Sparse Core Ops, SparseCore 0:
  44.7 57.5 all-reduce.4
  113.5 54.7 all-reduce.6
  203.3 54.7 all-reduce.8
  269.5 54.7 all-reduce.10
where the time goes:
time: 335 us; the launch traced here: 333 us
  waiting for transfers between devices  222 us (66%)
  matrix products  53.9 us (16%)
  other arithmetic  29.5 us (9%)
  between operations  13.7 us (4%)
  local copies, waits for them, and re-layouts  13.5 us (4%)
    psum x2, waiting for transfers between devices, decoder_layer(): attn_sum = lax.psum(attn_part, 'tp')  112 us
    psum x2, waiting for transfers between devices, decoder_layer(): mlp_sum = lax.psum(mlp_part, 'tp')  109 us
    dot_general x2, matrix products, decoder_layer(): jnp.dot(activated, w_down, preferred_element_type=jnp.float32)  12.6 us
    dot_general x2, matrix products, attention(): jnp.einsum('bgrs,bgsd->bgrd', dec_prob[..., :seq_len], v_cache[:dec_rows]...  11.5 us
    dot_general x2, matrix products, attention(): jnp.einsum('bgrd,bgsd->bgrs', q_dec, k_cache[:dec_rows], preferred_elemen...  9.2 us
  transfers between devices with their start and end apart: 4, of which 4 were waited for; matrix products, arithmetic and copies ran while one was open for 0% of the time, Pallas kernels for 0%

commit v1 on v0

--- a/solution.py
+++ b/solution.py
@@ -1,10 +1,16 @@
+import functools
+
 import jax
 import jax.numpy as jnp
 from jax import lax
+from jax.experimental import pallas as pl
+from jax.experimental.pallas import tpu as pltpu
 from jax.sharding import PartitionSpec as P
 
 ROPE_BASE = 500000.0
 EPSILON = 1e-5
+MESH = pl.DeviceIdType.MESH
+LANES = 128
 
 
 def rms_norm(x, norm_gain):
@@ -59,7 +65,139 @@
     return jnp.concatenate([dec_out.reshape(dec_rows, -1), chk_out.reshape(chunk_len, -1)], axis=0).astype(jnp.bfloat16)
 
 
-def decoder_layer(x, cos_tab, sin_tab, lengths, attn_gain, w_q, w_k, w_v, w_o, mlp_gain, w_gate, w_up, w_down, k_cache, v_cache):
+def sum_kernel(chips, part_ref, x_ref, out_ref, pair_in, pair_sum, ring_in, relay,
+               pair_send, pair_recv, ring_send, ring_recv, gather_send, gather_recv, share_send, share_recv):
+    me = lax.axis_index('tp')
+    core, chip = lax.rem(me, 2), lax.div(me, 2)
+    half = part_ref.shape[1] // 2
+    width = half // chips
+    sub = width // 2
+
+    def at_chip(step):
+        return lax.rem(chip + step + chips, chips)
+
+    partner = {'tp': chip * 2 + 1 - core}
+    right = {'tp': at_chip(1) * 2 + core}
+    left = {'tp': at_chip(-1) * 2 + core}
+
+    def columns(which_core, which_chip, part):
+        start = which_core * half + which_chip * width
+        if part == 2:
+            return pl.ds(pl.multiple_of(start, LANES), width)
+        return pl.ds(pl.multiple_of(start + part * sub, LANES), sub)
+
+    def copy(src, dst, send, recv, to):
+        return pltpu.make_async_remote_copy(src_ref=src, dst_ref=dst, send_sem=send, recv_sem=recv, device_id=to, device_id_type=MESH)
+
+    barrier = pltpu.get_barrier_semaphore()
+    for device in (partner, right, left):
+        pl.semaphore_signal(barrier, inc=1, device_id=device, device_id_type=MESH)
+    pl.semaphore_wait(barrier, 3)
+
+    steps = (2, 1, -1, 0)
+    pairs = []
+    for slot, step in enumerate(steps):
+        pairs.append(copy(part_ref.at[:, columns(1 - core, at_chip(step), 2)], pair_in.at[slot], pair_send.at[slot], pair_recv.at[slot], partner))
+        pairs[-1].start()
+
+    def pair_add(slot):
+        pairs[slot].wait_recv()
+        own = part_ref[:, columns(core, at_chip(steps[slot]), 2)].astype(jnp.float32)
+        return own + pair_in[slot].astype(jnp.float32)
+
+    def ring(src, slot, to):
+        ring_copy = copy(src, ring_in.at[slot], ring_send.at[slot], ring_recv.at[slot], to)
+        ring_copy.start()
+        return ring_copy
+
+    total = pair_add(0).astype(jnp.bfloat16)
+    pair_sum[0] = total[:, :sub]
+    pair_sum[1] = total[:, sub:]
+    rings = [None] * 6
+    rings[0] = ring(pair_sum.at[0], 0, right)
+    rings[3] = ring(pair_sum.at[1], 3, left)
+    ahead = pair_add(1)
+    pair_sum[2] = ahead[:, sub:].astype(jnp.bfloat16)
+    rings[1] = ring(pair_sum.at[2], 1, right)
+    behind = pair_add(2)
+    pair_sum[3] = behind[:, :sub].astype(jnp.bfloat16)
+    rings[4] = ring(pair_sum.at[3], 4, left)
+    rings[0].wait_recv()
+    relay[0] = (ahead[:, :sub] + ring_in[0].astype(jnp.float32)).astype(jnp.bfloat16)
+    rings[2] = ring(relay.at[0], 2, right)
+    rings[3].wait_recv()
+    relay[1] = (behind[:, sub:] + ring_in[3].astype(jnp.float32)).astype(jnp.bfloat16)
+    rings[5] = ring(relay.at[1], 5, left)
+    mine = pair_add(3) + x_ref[:, columns(core, chip, 2)].astype(jnp.float32)
+    rings[1].wait_recv()
+    rings[4].wait_recv()
+    first = mine[:, :sub] + ring_in[4].astype(jnp.float32)
+    second = mine[:, sub:] + ring_in[1].astype(jnp.float32)
+    rings[2].wait_recv()
+    out_ref[:, columns(core, chip, 0)] = (first + ring_in[2].astype(jnp.float32)).astype(jnp.bfloat16)
+
+    def gather(step, part, slot, dst_slot, to):
+        block = out_ref.at[:, columns(core, at_chip(step), part)]
+        gather_copy = copy(block, block, gather_send.at[slot], gather_recv.at[dst_slot], to)
+        gather_copy.start()
+        return gather_copy
+
+    def share(step, part, slot):
+        block = out_ref.at[:, columns(core, at_chip(step), part)]
+        share_copy = copy(block, block, share_send.at[slot], share_recv.at[slot], partner)
+        share_copy.start()
+        return share_copy
+
+    gathers = [None] * 6
+    gathers[0] = gather(0, 0, 0, 0, right)
+    rings[5].wait_recv()
+    out_ref[:, columns(core, chip, 1)] = (second + ring_in[5].astype(jnp.float32)).astype(jnp.bfloat16)
+    gathers[2] = gather(0, 1, 2, 2, left)
+    gathers[1] = gather(0, 1, 1, 1, right)
+    gathers[3] = gather(0, 0, 3, 3, left)
+    shares = [share(0, 2, 0)]
+    gathers[0].wait_recv()
+    gathers[4] = gather(-1, 0, 4, 4, right)
+    shares.append(share(-1, 0, 1))
+    gathers[2].wait_recv()
+    gathers[5] = gather(1, 1, 5, 5, left)
+    shares.append(share(1, 1, 2))
+    gathers[1].wait_recv()
+    shares.append(share(-1, 1, 3))
+    gathers[3].wait_recv()
+    shares.append(share(1, 0, 4))
+    gathers[4].wait_recv()
+    shares.append(share(2, 0, 5))
+    gathers[5].wait_recv()
+    shares.append(share(2, 1, 6))
+    for each in shares:
+        each.wait_recv()
+    for each in pairs + rings + gathers + shares:
+        each.wait_send()
+
+
+def add_sum(part, x, tp_size, collective_id):
+    rows, cols = part.shape
+    width = cols // tp_size
+    sub = width // 2
+    dma = pltpu.SemaphoreType.DMA
+    return pl.pallas_call(
+        functools.partial(sum_kernel, tp_size // 2),
+        out_shape=jax.ShapeDtypeStruct(part.shape, part.dtype),
+        in_specs=[pl.BlockSpec(memory_space=pltpu.VMEM)] * 2,
+        out_specs=pl.BlockSpec(memory_space=pltpu.VMEM),
+        scratch_shapes=[
+            pltpu.VMEM((4, rows, width), jnp.bfloat16),
+            pltpu.VMEM((4, rows, sub), jnp.bfloat16),
+            pltpu.VMEM((6, rows, sub), jnp.bfloat16),
+            pltpu.VMEM((2, rows, sub), jnp.bfloat16),
+            dma((4,)), dma((4,)), dma((6,)), dma((6,)), dma((6,)), dma((6,)), dma((7,)), dma((7,)),
+        ],
+        compiler_params=pltpu.CompilerParams(collective_id=collective_id, has_side_effects=True),
+    )(part, x)
+
+
+def decoder_layer(x, cos_tab, sin_tab, lengths, attn_gain, w_q, w_k, w_v, w_o, mlp_gain, w_gate, w_up, w_down, k_cache, v_cache, tp_size, layer_idx):
     head_dim = k_cache.shape[-1]
     normed = rms_norm(x, attn_gain)
     q_rot = apply_rope(project(normed, w_q, head_dim), cos_tab, sin_tab)
@@ -67,15 +205,13 @@
     v_new = project(normed, w_v, head_dim)
     attended = attention(q_rot, k_rot, v_new, k_cache, v_cache, lengths)
     attn_part = jnp.dot(attended, w_o, preferred_element_type=jnp.float32).astype(jnp.bfloat16)
-    attn_sum = lax.psum(attn_part, 'tp')
-    hidden = (x.astype(jnp.float32) + attn_sum.astype(jnp.float32)).astype(jnp.bfloat16)
+    hidden = add_sum(attn_part, x, tp_size, 2 * layer_idx)
     mlp_in = rms_norm(hidden, mlp_gain)
     gate_proj = jnp.dot(mlp_in, w_gate, preferred_element_type=jnp.float32)
     up_proj = jnp.dot(mlp_in, w_up, preferred_element_type=jnp.float32)
     activated = (jax.nn.silu(gate_proj) * up_proj).astype(jnp.bfloat16)
     mlp_part = jnp.dot(activated, w_down, preferred_element_type=jnp.float32).astype(jnp.bfloat16)
-    mlp_sum = lax.psum(mlp_part, 'tp')
-    return (hidden.astype(jnp.float32) + mlp_sum.astype(jnp.float32)).astype(jnp.bfloat16)
+    return add_sum(mlp_part, hidden, tp_size, 2 * layer_idx + 1)
 
 
 def solution(mesh):
@@ -83,6 +219,7 @@
     row_spec = P(None, 'tp', None)
     cache_spec = P(None, 'dp', 'tp', None, None)
     in_specs = (P('dp', None), P('dp'), P(), col_spec, col_spec, col_spec, row_spec, P(), col_spec, col_spec, row_spec, cache_spec, cache_spec)
+    tp_size = mesh.shape['tp']
 
     def body(x, lengths, attn_gain, w_q, w_k, w_v, w_o, mlp_gain, w_gate, w_up, w_down, k_cache, v_cache):
         dec_rows = lengths.shape[0] - 1
@@ -91,7 +228,7 @@
         cos_tab, sin_tab = rope_tables(positions, k_cache.shape[-1])
         hidden = x
         for layer_idx in range(w_q.shape[0]):
-            hidden = decoder_layer(hidden, cos_tab, sin_tab, lengths, attn_gain[layer_idx], w_q[layer_idx], w_k[layer_idx], w_v[layer_idx], w_o[layer_idx], mlp_gain[layer_idx], w_gate[layer_idx], w_up[layer_idx], w_down[layer_idx], k_cache[layer_idx], v_cache[layer_idx])
+            hidden = decoder_layer(hidden, cos_tab, sin_tab, lengths, attn_gain[layer_idx], w_q[layer_idx], w_k[layer_idx], w_v[layer_idx], w_o[layer_idx], mlp_gain[layer_idx], w_gate[layer_idx], w_up[layer_idx], w_down[layer_idx], k_cache[layer_idx], v_cache[layer_idx], tp_size, layer_idx)
         return hidden
 
     return jax.shard_map(body, mesh=mesh, in_specs=in_specs, out_specs=P('dp', None), check_vma=False)

time: 335 us -> 181 us (0.54)
  waiting for transfers between devices: 222 us -> 0 us
  Pallas kernels: 0 us -> 82.1 us
  between operations: 13.7 us -> 0.55 us
  matrix products: 53.9 us -> 57.8 us
    psum x4 -> x0, waiting for transfers between devices: 222 us -> none  [the longest x2 112 us: decoder_layer(): attn_sum = lax.psum(attn_part, 'tp')]
    pallas_call x0 -> x4, Pallas kernels: none -> 82.1 us  [add_sum(): pl.pallas_call(functools.partial(sum_kernel, tp_size // 2), out_shape=jax...]
    dot_general x6, matrix products: 3.91 us -> 7.38 us  [project(): jnp.dot(normed, weight, preferred_element_type=jnp.float32)]
  transfers between devices with their start and end apart: 4 -> 0, of which waited for: 4 -> 0; matrix products, arithmetic and copies ran while one was open for 0% -> 0% of each run, Pallas kernels for 0% -> 0%
where the time goes in v1:
time: 181 us; the launch traced here: 179 us
  Pallas kernels  82.1 us (45%)
  matrix products  57.8 us (32%)
  other arithmetic  26.6 us (15%)
  local copies, waits for them, and re-layouts  12.5 us (7%)
    pallas_call x4, Pallas kernels, add_sum(): pl.pallas_call(functools.partial(sum_kernel, tp_size // 2), out_shape=jax...  82.1 us
    dot_general x2, matrix products, decoder_layer(): jnp.dot(activated, w_down, preferred_element_type=jnp.float32)  12.7 us
    dot_general x2, matrix products, attention(): jnp.einsum('bgrs,bgsd->bgrd', dec_prob[..., :seq_len], v_cache[:dec_rows]...  11.3 us
    dot_general x2, matrix products, attention(): jnp.einsum('bgrd,bgsd->bgrs', q_dec, k_cache[:dec_rows], preferred_elemen...  9.2 us
    dot_general x6, matrix products, project(): jnp.dot(normed, weight, preferred_element_type=jnp.float32)  7.38 us
    dot_general x2, matrix products, decoder_layer(): gate_proj = jnp.dot(mlp_in, w_gate, preferred_element_type=jnp.float32)  7.06 us
    reduce_sum x4, other arithmetic, rms_norm(): jnp.mean(x_f32 * x_f32, axis=-1, keepdims=True) + EPSILON  5.56 us
    concatenate x2, other arithmetic, attention(): jnp.concatenate([dec_cache, dec_self], axis=-1)  5.47 us

profile of v1, /device:TPU:81, one launch (start us, length us, event | category | flops | bytes accessed | tf_op | source)
XLA Modules:
  0.0 179.5 jit_solution(1903198282420936850)
XLA Ops:
  6.4 1.6 convolution_convert_fusion.6
  9.0 1.7 fusion.67
  13.1 4.6 %fusion.3 = f32[64,4,1024]{2,1,0:T(4,128)S(1)} fusion(bf16[192,4,64]{2,1,0:T(4,128)(2,1)S(1)} %pad_maximum_fusion, bf16[2,65,1,1024,64]{3,4,1,2,0:T(8,128)(2,1)} %bitcast.262), kind=kOutput, calls=%fused_computation.7 | convolution fusion | flops 33554432 | bytes 9535488 | tf_op jit(solution)/shard_map/bgrd,bgsd->bgrs/dot_general | solution.py:52
  17.7 1.8 %copy.115 = f32[64,4,1024]{0,1,2:T(4,128)} copy(f32[64,4,1024]{2,1,0:T(4,128)S(1)} %fusion.3) | data formatting | bytes 2097152 | tf_op jit(solution)/shard_map/bgrd,bgsd->bgrs/dot_general | solution.py:52
  19.5 2.7 %fusion.37 = (f32[64,1,4,1024]{0,2,3,1:T(4,128)S(1)}, f32[64,4]{0,1:T(4,128)S(1)}) fusion(f32[64,4,1024]{0,1,2:T(4,128)} %copy.115, pred[64,1024]{0,1:T(8,128)(4,1)S(1)} %iota_compare_fusion), kind=kLoop, calls=%fused_computation.59 | loop fusion | flops 786176 | bytes 2163712 | tf_op jit(solution)/shard_map/concatenate | solution.py:55
  22.5 2.0 %fusion.89 = f32[64,4]{0,1:T(4,128)S(1)} fusion(f32[64,4]{0,1:T(4,128)S(1)} %copy.118, f32[64,1,4,1]{0,2,3,1:T(4,128)S(1)} %bitcast.248, f32[64,1,4,1024]{0,2,3,1:T(4,128)S(1)} %get-tuple-element.7), kind=kLoop, calls=%fused_computation.119 | loop fusion | flops 786944 | bytes 1051648 | tf_op jit(solution)/shard_map/reduce_sum | solution.py:55
  24.5 1.8 %divide_convert_fusion.3 = bf16[64,1,4,1025]{0,2,3,1:T(4,128)(2,1)S(1)} fusion(f32[64,4]{0,1:T(4,128)S(1)} %fusion.89, f32[64,4]{0,1:T(4,128)S(1)} %copy.118, f32[64,1,4,1]{0,2,3,1:T(4,128)S(1)} %bitcast.249, f32[64,1,4,1024]{0,2,3,1:T(4,128)S(1)} %get-tuple-element.7), kind=kLoop, calls=%fused_computation.41 | loop fusion | flops 1049600 | bytes 1576448 | tf_op jit(solution)/shard_map/convert_element_type | solution.py:55
  27.8 5.6 %fusion.73 = bf16[64,4,64]{2,1,0:T(4,128)(2,1)S(1)} fusion(bf16[64,4,1024]{2,1,0:T(4,128)(2,1)S(1)} %copy.120, bf16[2,65,1,1024,64]{3,4,1,2,0:T(8,128)(2,1)} %bitcast.266, f32[64,64]{1,0:T(8,128)S(1)} %copy.122, f32[64,4]{1,0:T(8,128)S(1)} %copy.121), kind=kOutput, calls=%fused_computation.95 | convolution fusion | flops 33603584 | bytes 8963072 | tf_op jit(solution)/shard_map/bgrs,bgsd->bgrd/dot_general | solution.py:56
  39.1 22.7 %shard_map.127.x_ref = bf16[192,2048]{1,0:T(8,128)(2,1)} custom-call(bf16[192,2048]{1,0:T(8,128)(2,1)} %convolution_convert_fusion.1.part_ref, bf16[192,2048]{1,0:T(8,128)(2,1)} %x_ref.1), custom_call_target="tpu_custom_call" | custom-call | tf_op jit(solution)/shard_map/pallas_call | solution.py:184
  63.2 3.5 %fusion.14 = f32[192,1024]{1,0:T(8,128)S(1)} fusion(bf16[2,2048,1024]{2,1,0:T(8,128)(2,1)} %param.21, bf16[192,2048]{1,0:T(8,128)(2,1)} %shard_map.127.x_ref, f32[2048]{0:T(1024)S(1)} %bitcast.257, f32[192]{0:T(256)S(1)} %add_rsqrt_fusion.2), kind=kOutput, calls=%fused_computation.18 | convolution fusion | flops 806879232 | bytes 5776128 | tf_op jit(solution)/shard_map/dot_general | solution.py:210
  66.7 6.3 %fusion.22.part_ref = bf16[192,2048]{1,0:T(8,128)(2,1)} fusion(bf16[2,1024,2048]{2,1,0:T(8,128)(2,1)} %param.23, bf16[2,2048,1024]{2,1,0:T(8,128)(2,1)} %param.22, f32[192,1024]{1,0:T(8,128)S(1)} %fusion.14, bf16[192,2048]{1,0:T(8,128)(2,1)S(1)} %copy-done.2, f32[2048]{0:T(1024)S(1)} %bitcast.258, f32[192]{0:T(256)S(1)} %add_rsqrt_fusion.2), kind=kOutput, calls=%fused_computation.26 | convolution fusion | flops 1613758464 | bytes 10756864 | tf_op jit(solution)/shard_map/dot_general | solution.py:213
  73.0 19.2 %shard_map.128.x_ref = bf16[192,2048]{1,0:T(8,128)(2,1)} custom-call(bf16[192,2048]{1,0:T(8,128)(2,1)} %fusion.22.part_ref, bf16[192,2048]{1,0:T(8,128)(2,1)} %shard_map.127.x_ref), custom_call_target="tpu_custom_call" | custom-call | tf_op jit(solution)/shard_map/pallas_call | solution.py:184
  96.2 1.6 fusion.66
  99.8 4.6 %fusion.1 = f32[64,4,1024]{2,1,0:T(4,128)S(1)} fusion(bf16[192,4,64]{2,1,0:T(4,128)(2,1)S(1)} %pad_maximum_fusion.1, bf16[2,65,1,1024,64]{3,4,1,2,0:T(8,128)(2,1)} %bitcast.263), kind=kOutput, calls=%fused_computation.3 | convolution fusion | flops 33554432 | bytes 9535488 | tf_op jit(solution)/shard_map/bgrd,bgsd->bgrs/dot_general | solution.py:52
  104.4 2.0 %copy.131 = f32[64,4,1024]{0,1,2:T(4,128)} copy(f32[64,4,1024]{2,1,0:T(4,128)S(1)} %fusion.1) | data formatting | bytes 2097152 | tf_op jit(solution)/shard_map/bgrd,bgsd->bgrs/dot_general | solution.py:52
  106.5 2.7 %fusion.39 = (f32[64,1,4,1024]{0,2,3,1:T(4,128)S(1)}, f32[64,4]{0,1:T(4,128)S(1)}) fusion(f32[64,4,1024]{0,1,2:T(4,128)} %copy.131, pred[64,1024]{0,1:T(8,128)(4,1)S(1)} %iota_compare_fusion), kind=kLoop, calls=%fused_computation.61 | loop fusion | flops 786176 | bytes 2163712 | tf_op jit(solution)/shard_map/concatenate | solution.py:55
  109.5 2.0 %fusion.88 = f32[64,4]{0,1:T(4,128)S(1)} fusion(f32[64,4]{0,1:T(4,128)S(1)} %copy.134, f32[64,1,4,1]{0,2,3,1:T(4,128)S(1)} %bitcast.250, f32[64,1,4,1024]{0,2,3,1:T(4,128)S(1)} %get-tuple-element.5), kind=kLoop, calls=%fused_computation.118 | loop fusion | flops 786944 | bytes 1051648 | tf_op jit(solution)/shard_map/reduce_sum | solution.py:55
  111.4 1.8 %divide_convert_fusion.2 = bf16[64,1,4,1025]{0,2,3,1:T(4,128)(2,1)S(1)} fusion(f32[64,4]{0,1:T(4,128)S(1)} %fusion.88, f32[64,4]{0,1:T(4,128)S(1)} %copy.134, f32[64,1,4,1]{0,2,3,1:T(4,128)S(1)} %bitcast.251, f32[64,1,4,1024]{0,2,3,1:T(4,128)S(1)} %get-tuple-element.5), kind=kLoop, calls=%fused_computation.40 | loop fusion | flops 1049600 | bytes 1576448 | tf_op jit(solution)/shard_map/convert_element_type | solution.py:55
  114.5 5.6 %fusion.72 = bf16[64,4,64]{2,1,0:T(4,128)(2,1)S(1)} fusion(bf16[64,4,1024]{2,1,0:T(4,128)(2,1)S(1)} %copy.136, bf16[2,65,1,1024,64]{3,4,1,2,0:T(8,128)(2,1)} %bitcast.267, f32[64,64]{1,0:T(8,128)S(1)} %copy.138, f32[64,4]{1,0:T(8,128)S(1)} %copy.137), kind=kOutput, calls=%fused_computation.94 | convolution fusion | flops 33603584 | bytes 8963072 | tf_op jit(solution)/shard_map/bgrs,bgsd->bgrd/dot_general | solution.py:56
  125.9 21.7 %shard_map.129.x_ref = bf16[192,2048]{1,0:T(8,128)(2,1)} custom-call(bf16[192,2048]{1,0:T(8,128)(2,1)} %convolution_convert_fusion.part_ref, bf16[192,2048]{1,0:T(8,128)(2,1)} %shard_map.128.x_ref), custom_call_target="tpu_custom_call" | custom-call | tf_op jit(solution)/shard_map/pallas_call | solution.py:184
  148.9 3.5 %fusion.8 = f32[192,1024]{1,0:T(8,128)S(1)} fusion(bf16[2,2048,1024]{2,1,0:T(8,128)(2,1)} %param.21, bf16[192,2048]{1,0:T(8,128)(2,1)} %shard_map.129.x_ref, f32[2048]{0:T(1024)S(1)} %bitcast.252, f32[192]{0:T(256)S(1)} %add_rsqrt_fusion), kind=kOutput, calls=%fused_computation.12 | convolution fusion | flops 806879232 | bytes 5776128 | tf_op jit(solution)/shard_map/dot_general | solution.py:210
  152.5 6.4 %fusion.25.part_ref = bf16[192,2048]{1,0:T(8,128)(2,1)} fusion(bf16[2,1024,2048]{2,1,0:T(8,128)(2,1)} %param.23, bf16[2,2048,1024]{2,1,0:T(8,128)(2,1)} %param.22, f32[192,1024]{1,0:T(8,128)S(1)} %fusion.8, bf16[192,2048]{1,0:T(8,128)(2,1)S(1)} %copy-done.1, f32[2048]{0:T(1024)S(1)} %bitcast.253, f32[192]{0:T(256)S(1)} %add_rsqrt_fusion), kind=kOutput, calls=%fused_computation.27 | convolution fusion | flops 1613758464 | bytes 10756864 | tf_op jit(solution)/shard_map/dot_general | solution.py:213
  158.8 18.5 %shard_map.130 = bf16[192,2048]{1,0:T(8,128)(2,1)} custom-call(bf16[192,2048]{1,0:T(8,128)(2,1)} %fusion.25.part_ref, bf16[192,2048]{1,0:T(8,128)(2,1)} %shard_map.129.x_ref), custom_call_target="tpu_custom_call" | custom-call | tf_op jit(solution)/shard_map/pallas_call | solution.py:184
  177.4 2.1 %copy.158 = bf16[192,2048]{1,0:T(8,128)(2,1)} copy(bf16[192,2048]{1,0:T(8,128)(2,1)} %shard_map.130) | data formatting | bytes 1572864
  (103 shorter events, 32.7 us)
Async XLA Ops:
  0.0 8.1 %copy-start.3 = (bf16[192,2048]{1,0:T(8,128)(2,1)S(1)}, bf16[192,2048]{1,0:T(8,128)(2,1)}, u32[]{:S(2)}) copy-start(bf16[192,2048]{1,0:T(8,128)(2,1)} %x_ref.1) | copy-start | bytes 2359300
  0.0 8.1 %copy-start.8 = (bf16[2,2048,64]{1,2,0:T(8,128)(2,1)S(1)}, bf16[2,2048,64]{1,2,0:T(8,128)(2,1)}, u32[]{:S(2)}) copy-start(bf16[2,2048,64]{1,2,0:T(8,128)(2,1)} %param.17) | copy-start | bytes 1572868
  4.8 4.1 %copy-start.6 = (s32[65]{0:T(128)S(1)}, s32[65]{0:T(128)}, u32[]{:S(2)}) copy-start(s32[65]{0:T(128)} %param.14) | copy-start | bytes 784
  35.5 2.2 %copy-start.4 = (bf16[2,256,2048]{2,1,0:T(8,128)(2,1)S(1)}, bf16[2,256,2048]{2,1,0:T(8,128)(2,1)}, u32[]{:S(2)}) copy-start(bf16[2,256,2048]{2,1,0:T(8,128)(2,1)} %param.19) | copy-start | bytes 6291460
  63.2 3.5 %copy-start.2 = (bf16[192,2048]{1,0:T(8,128)(2,1)S(1)}, bf16[192,2048]{1,0:T(8,128)(2,1)}, u32[]{:S(2)}) copy-start(bf16[192,2048]{1,0:T(8,128)(2,1)} %shard_map.127.x_ref) | copy-start | bytes 2359300
  73.0 20.7 %copy-start.7 = (bf16[2,2048,64]{1,2,0:T(8,128)(2,1)S(1)}, bf16[2,2048,64]{1,2,0:T(8,128)(2,1)}, u32[]{:S(2)}) copy-start(bf16[2,2048,64]{1,2,0:T(8,128)(2,1)} %param.18) | copy-start | bytes 1572868
  73.0 22.4 %copy-start.9 = (bf16[2,2048,64]{1,2,0:T(8,128)(2,1)S(1)}, bf16[2,2048,64]{1,2,0:T(8,128)(2,1)}, u32[]{:S(2)}) copy-start(bf16[2,2048,64]{1,2,0:T(8,128)(2,1)} %param.17) | copy-start | bytes 1572868
  92.2 3.1 %copy-start = (bf16[192,2048]{1,0:T(8,128)(2,1)S(1)}, bf16[192,2048]{1,0:T(8,128)(2,1)}, u32[]{:S(2)}) copy-start(bf16[192,2048]{1,0:T(8,128)(2,1)} %shard_map.128.x_ref) | copy-start | bytes 2359300
  122.3 2.2 %copy-start.5 = (bf16[2,256,2048]{2,1,0:T(8,128)(2,1)S(1)}, bf16[2,256,2048]{2,1,0:T(8,128)(2,1)}, u32[]{:S(2)}) copy-start(bf16[2,256,2048]{2,1,0:T(8,128)(2,1)} %param.19) | copy-start | bytes 6291460
  148.9 3.5 %copy-start.1 = (bf16[192,2048]{1,0:T(8,128)(2,1)S(1)}, bf16[192,2048]{1,0:T(8,128)(2,1)}, u32[]{:S(2)}) copy-start(bf16[192,2048]{1,0:T(8,128)(2,1)} %shard_map.129.x_ref) | copy-start | bytes 2359300

commit v2 on v0

v2 whole, which is shorter than its diff:
```python
import functools

import jax
import jax.numpy as jnp
from jax import lax
from jax.experimental import pallas as pl
from jax.experimental.pallas import tpu as pltpu
from jax.sharding import PartitionSpec as P

ROPE_BASE = 500000.0
EPSILON = 1e-5
MESH = pl.DeviceIdType.MESH
LANES = 128
SEQS = 8
VMEM_LIMIT = 67043328
F32 = jnp.float32
BF16 = jnp.bfloat16
NT = (((1,), (1,)), ((), ()))


def matmul(a, b):
    return jnp.dot(a, b, preferred_element_type=F32)


def matmul_nt(a, b):
    return lax.dot_general(a, b, NT, preferred_element_type=F32)


def layer_kernel(chips, x_ref, lens_ref, freq_ref, again_ref, mgain_ref, wq_hbm, wk_hbm, wv_hbm, wo_hbm, wg_hbm, wu_hbm, wd_hbm, k_hbm, v_hbm,
                 out_ref,
                 wq, wkv, wo, wg, wu, wd, kbuf, vbuf, hid, normed, act, part, lens_v, cos_t, sin_t, q_t, k_t, v_t, self_t, qbd, qh, oh, att,
                 pair_in, pair_sum, ring_in, relay,
                 load_sem, cache_sem, pair_send, pair_recv, ring_send, ring_recv, gather_send, gather_recv, share_send, share_recv):
    layers = wq.shape[0]
    rows, cols = x_ref.shape
    dec = lens_v.shape[0]
    chunk = rows - dec
    head = k_hbm.shape[2]
    seq_len = k_hbm.shape[3]
    scale = head ** -0.5
    groups = dec // SEQS
    half = cols // 2
    width = half // chips
    sub = width // 2

    me = lax.axis_index('tp')
    core, chip = lax.rem(me, 2), lax.div(me, 2)

    def at_chip(step):
        return lax.rem(chip + step + chips, chips)

    partner = {'tp': chip * 2 + 1 - core}
    right = {'tp': at_chip(1) * 2 + core}
    left = {'tp': at_chip(-1) * 2 + core}

    def weight_loads(layer, names):
        table = {
            'q': [(wq_hbm.at[layer], wq.at[layer], 0)],
            'kv': [(wk_hbm.at[layer], wkv.at[layer, 0:head], 1), (wk_hbm.at[layer], wkv.at[layer, head:2 * head], 2),
                   (wv_hbm.at[layer], wkv.at[layer, 2 * head:3 * head], 3), (wv_hbm.at[layer], wkv.at[layer, 3 * head:4 * head], 4)],
            'o': [(wo_hbm.at[layer], wo.at[layer], 5)],
            'g': [(wg_hbm.at[layer], wg.at[layer], 6)],
            'u': [(wu_hbm.at[layer], wu.at[layer], 7)],
            'd': [(wd_hbm.at[layer], wd.at[layer], 8)],
        }
        return [pltpu.make_async_copy(src, dst, load_sem.at[layer, slot]) for name in names for src, dst, slot in table[name]]

    def group_load(layer, which, group):
        src, dst = ((k_hbm, kbuf), (v_hbm, vbuf))[which]
        block = pl.ds(group * SEQS, SEQS)
        return pltpu.make_async_copy(src.at[layer, block], dst.at[block], cache_sem.at[layer, which, group])

    def chunk_load(layer, which):
        src, dst = ((k_hbm, kbuf), (v_hbm, vbuf))[which]
        return pltpu.make_async_copy(src.at[layer, dec], dst.at[dec], cache_sem.at[layer, which, groups])

    def start(copies):
        for each in copies:
            each.start()

    def wait(copies):
        for each in copies:
            each.wait()

    def start_caches(layer):
        start([chunk_load(layer, 0), chunk_load(layer, 1)])

        def issue(group, carry):
            group_load(layer, 0, group).start()
            group_load(layer, 1, group).start()
            return carry

        lax.fori_loop(0, groups, issue, 0)

    start(weight_loads(0, ('q', 'kv')))
    start_caches(0)
    start(weight_loads(0, ('o', 'g', 'u', 'd')))

    barrier = pltpu.get_barrier_semaphore()
    for device in (partner, right, left):
        pl.semaphore_signal(barrier, inc=1, device_id=device, device_id_type=MESH)

    def fill(row, carry):
        lens_v[pl.ds(row, 1), :] = jnp.full((1, LANES), lens_ref[row], jnp.int32)
        return carry

    lax.fori_loop(0, dec, fill, 0)

    def table(row, positions):
        angles = positions.astype(F32) * freq_ref[0:1, :]
        cos_t[pl.ds(row, 8), :] = jnp.cos(angles)
        sin_t[pl.ds(row, 8), :] = jnp.sin(angles)

    def dec_table(i, carry):
        row = pl.multiple_of(i * 8, 8)
        table(row, lens_v[pl.ds(row, 8), :])
        return carry

    def chunk_table(i, carry):
        row = pl.multiple_of(i * 8, 8)
        table(dec + row, lens_ref[dec] + row + lax.broadcasted_iota(jnp.int32, (8, LANES), 0))
        return carry

    lax.fori_loop(0, dec // 8, dec_table, 0)
    lax.fori_loop(0, chunk // 8, chunk_table, 0)

    def normalize(src, gain):
        def block(i, carry):
            band = pl.ds(pl.multiple_of(i * 16, 16), 16)
            values = src[band, :].astype(F32)
            inv = lax.rsqrt(jnp.sum(values * values, axis=1, keepdims=True) * (1.0 / cols) + EPSILON)
            normed[band, :] = (values * inv * gain).astype(BF16)
            return carry

        lax.fori_loop(0, rows // 16, block, 0)

    def rope(values):
        wide = values.shape[1]
        lane = lax.broadcasted_iota(jnp.int32, values.shape, 1)
        turned = jnp.where(lane % head < head // 2, -pltpu.roll(values, wide - head // 2, 1), pltpu.roll(values, head // 2, 1))
        cos, sin = cos_t[...], sin_t[...]
        if wide > LANES:
            cos, sin = jnp.concatenate([cos, cos], axis=1), jnp.concatenate([sin, sin], axis=1)
        return (values * cos + turned * sin).astype(BF16).astype(F32)

    def project(layer):
        q_t[...] = rope(matmul(normed[...], wq[layer]).astype(BF16).astype(F32))
        kv = matmul_nt(normed[...], wkv[layer]).astype(BF16)
        k_t[...] = rope(kv[:, :LANES].astype(F32))
        v_t[...] = kv[:, LANES:].astype(F32)

    def decode_setup():
        lane = lax.broadcasted_iota(jnp.int32, (dec, LANES), 1)
        keys = k_t[0:dec, :]
        for pair in range(2):
            block = q_t[0:dec, pair * LANES:(pair + 1) * LANES]
            swapped = pltpu.roll(block, head, 1)
            product = block * keys
            for side in range(2):
                r = 2 * pair + side
                mine = (lane < head) if side == 0 else (lane >= head)
                self_t[r] = jnp.broadcast_to(jnp.sum(jnp.where(mine, product, 0.0), axis=1, keepdims=True) * scale, (dec, LANES))
                twice = jnp.where(mine, block, swapped)
                wide = jnp.concatenate([twice] * (SEQS * head // LANES), axis=1)
                col = lax.broadcasted_iota(jnp.int32, wide.shape, 1)
                row = lax.broadcasted_iota(jnp.int32, wide.shape, 0)
                qbd[r] = jnp.where(col // head == row % SEQS, wide, 0.0)

    def decode(layer):
        def group_step(group, carry):
            band = pl.ds(pl.multiple_of(group * SEQS, SEQS), SEQS)
            heads = qbd.shape[0]
            queries = qbd[:, band, :].reshape(heads * SEQS, SEQS * head).astype(BF16)
            group_load(layer, 0, group).wait()
            logits = matmul(queries, kbuf[pl.ds(group * SEQS, SEQS)].reshape(SEQS * head, seq_len)) * scale
            logits = logits.reshape(heads, SEQS, seq_len)
            seen = lax.broadcasted_iota(jnp.int32, (SEQS, seq_len), 1) < lens_v[band, 0:1]
            logits = jnp.where(seen[None], logits, -jnp.inf)
            own = self_t[:, band, 0:1]
            top = jnp.maximum(jnp.max(logits, axis=2, keepdims=True), own)
            weights = jnp.exp(logits - top)
            own_weight = jnp.exp(own - top)
            inv = 1.0 / (jnp.sum(weights, axis=2, keepdims=True) + own_weight)
            probs = (weights * inv).astype(BF16).reshape(heads * SEQS, seq_len)
            own_prob = (own_weight * inv).astype(BF16).astype(F32)
            group_load(layer, 1, group).wait()
            mixed = matmul_nt(probs, vbuf[pl.ds(group * SEQS, SEQS)].reshape(SEQS * head, seq_len))
            col = lax.broadcasted_iota(jnp.int32, mixed.shape, 1)
            row = lax.broadcasted_iota(jnp.int32, mixed.shape, 0)
            mixed = jnp.where(col // head == row % SEQS, mixed, 0.0)
            folded = mixed[:, 0:LANES]
            for i in range(1, SEQS * head // LANES):
                folded = folded + mixed[:, i * LANES:(i + 1) * LANES]
            folded = folded + pltpu.roll(folded, head, 1)
            result = folded.reshape(heads, SEQS, LANES) + own_prob * v_t[band, :][None]
            lane = lax.broadcasted_iota(jnp.int32, (SEQS, LANES), 1)
            att[band, 0:LANES] = jnp.where(lane < head, result[0], result[1])
            att[band, LANES:2 * LANES] = jnp.where(lane < head, result[2], result[3])
            return carry

        lax.fori_loop(0, groups, group_step, 0, unroll=2)

    def prefill(layer):
        lane = lax.broadcasted_iota(jnp.int32, (chunk, LANES), 1)
        for pair in range(2):
            block = q_t[dec:rows, pair * LANES:(pair + 1) * LANES]
            qh[2 * pair] = jnp.where(lane < head, block, 0.0).astype(BF16)
            qh[2 * pair + 1] = jnp.where(lane >= head, block, 0.0).astype(BF16)
        wait([chunk_load(layer, 0), chunk_load(layer, 1)])

        def head_step(r, carry):
            queries = qh[r]
            keys = kbuf[dec]
            logits = matmul(queries, jnp.concatenate([keys, keys], axis=0)) * scale
            seen = lax.broadcasted_iota(jnp.int32, (chunk, seq_len), 1) < lens_ref[dec]
            logits = jnp.where(seen, logits, -jnp.inf)
            own = matmul_nt(queries, k_t[dec:rows, :].astype(BF16)) * scale
            causal = lax.broadcasted_iota(jnp.int32, (chunk, chunk), 1) <= lax.broadcasted_iota(jnp.int32, (chunk, chunk), 0)
            own = jnp.where(causal, own, -jnp.inf)
            top = jnp.maximum(jnp.max(logits, axis=1, keepdims=True), jnp.max(own, axis=1, keepdims=True))
            weights = jnp.exp(logits - top)
            own_weights = jnp.exp(own - top)
            inv = 1.0 / (jnp.sum(weights, axis=1, keepdims=True) + jnp.sum(own_weights, axis=1, keepdims=True))
            probs = (weights * inv).astype(BF16)
            own_probs = (own_weights * inv).astype(BF16)
            values = vbuf[dec]
            oh[r] = matmul_nt(probs, jnp.concatenate([values, values], axis=0)) + matmul(own_probs, v_t[dec:rows, :].astype(BF16))
            return carry

        lax.fori_loop(0, qh.shape[0], head_step, 0)
        for pair in range(2):
            att[dec:rows, pair * LANES:(pair + 1) * LANES] = jnp.where(lane < head, oh[2 * pair], oh[2 * pair + 1])

    def copy(src, dst, send, recv, to):
        return pltpu.make_async_remote_copy(src_ref=src, dst_ref=dst, send_sem=send, recv_sem=recv, device_id=to, device_id_type=MESH)

    def step_of(slot):
        high, low = slot // 2, slot % 2
        return 2 - low + high * (1 - 2 * low)

    pending = []

    def sum_over_tp(index, product, base, target):
        def piece_of(which_core, slot):
            return which_core * chips + at_chip(step_of(slot))

        def pair_copy(slot):
            piece = piece_of(1 - core, slot)
            return copy(part.at[piece], pair_in.at[index, slot], pair_send.at[index, slot], pair_recv.at[index, slot], partner)

        def theirs(slot, carry):
            piece = piece_of(1 - core, slot)
            part[piece] = product(piece).astype(BF16)
            pair_copy(slot).start()
            return carry

        def ours(slot, carry):
            piece = piece_of(core, slot)
            part[piece] = product(piece).astype(BF16)
            return carry

        lax.fori_loop(0, 4, theirs, 0)
        lax.fori_loop(0, 4, ours, 0)

        def columns(which_core, which_chip, side):
            begin = which_core * half + which_chip * width
            if side == 2:
                return pl.ds(pl.multiple_of(begin, LANES), width)
            return pl.ds(pl.multiple_of(begin + side * sub, LANES), sub)

        def pair_add(slot):
            pair_copy(slot).wait_recv()
            return part[piece_of(core, slot)].astype(F32) + pair_in[index, slot].astype(F32)

        sent = []

        def ring(src, slot, to):
            ring_copy = copy(src, ring_in.at[index, slot], ring_send.at[index, slot], ring_recv.at[index, slot], to)
            ring_copy.start()
            sent.append(ring_copy)
            return ring_copy

        far = pair_add(0).astype(BF16)
        pair_sum[index, 0] = far[:, :sub]
        pair_sum[index, 1] = far[:, sub:]
        ring0 = ring(pair_sum.at[index, 0], 0, right)
        ring3 = ring(pair_sum.at[index, 1], 3, left)
        ahead = pair_add(1)
        pair_sum[index, 2] = ahead[:, sub:].astype(BF16)
        ring1 = ring(pair_sum.at[index, 2], 1, right)
        behind = pair_add(2)
        pair_sum[index, 3] = behind[:, :sub].astype(BF16)
        ring4 = ring(pair_sum.at[index, 3], 4, left)
        ring0.wait_recv()
        relay[index, 0] = (ahead[:, :sub] + ring_in[index, 0].astype(F32)).astype(BF16)
        ring2 = ring(relay.at[index, 0], 2, right)
        ring3.wait_recv()
        relay[index, 1] = (behind[:, sub:] + ring_in[index, 3].astype(F32)).astype(BF16)
        ring5 = ring(relay.at[index, 1], 5, left)
        mine = pair_add(3) + base[:, columns(core, chip, 2)].astype(F32)
        ring1.wait_recv()
        ring4.wait_recv()
        first = mine[:, :sub] + ring_in[index, 4].astype(F32)
        second = mine[:, sub:] + ring_in[index, 1].astype(F32)
        ring2.wait_recv()
        target[:, columns(core, chip, 0)] = (first + ring_in[index, 2].astype(F32)).astype(BF16)

        def gather(step, side, slot, to):
            block = target.at[:, columns(core, at_chip(step), side)]
            gather_copy = copy(block, block, gather_send.at[index, slot], gather_recv.at[index, slot], to)
            gather_copy.start()
            sent.append(gather_copy)
            return gather_copy

        shares = []

        def share(step, side, slot):
            block = target.at[:, columns(core, at_chip(step), side)]
            share_copy = copy(block, block, share_send.at[index, slot], share_recv.at[index, slot], partner)
            share_copy.start()
            sent.append(share_copy)
            shares.append(share_copy)

        gather0 = gather(0, 0, 0, right)
        ring5.wait_recv()
        target[:, columns(core, chip, 1)] = (second + ring_in[index, 5].astype(F32)).astype(BF16)
        gather2 = gather(0, 1, 2, left)
        gather1 = gather(0, 1, 1, right)
        gather3 = gather(0, 0, 3, left)
        share(0, 2, 0)
        gather0.wait_recv()
        gather4 = gather(-1, 0, 4, right)
        share(-1, 0, 1)
        gather2.wait_recv()
        gather5 = gather(1, 1, 5, left)
        share(1, 1, 2)
        gather1.wait_recv()
        share(-1, 1, 3)
        gather3.wait_recv()
        share(1, 0, 4)
        gather4.wait_recv()
        share(2, 0, 5)
        gather5.wait_recv()
        share(2, 1, 6)
        for each in shares:
            each.wait_recv()
        for slot in range(4):
            pair_copy(slot).wait_send()
        for each in sent:
            each.wait_send()

    def piece_columns(piece):
        return pl.ds(pl.multiple_of(piece * width, LANES), width)

    residual = x_ref
    for layer in range(layers):
        normalize(residual, again_ref[...].astype(F32)[layer:layer + 1])
        wait(weight_loads(layer, ('q', 'kv')))
        project(layer)
        decode_setup()
        decode(layer)
        prefill(layer)
        if layer + 1 < layers:
            start_caches(layer + 1)
            start(weight_loads(layer + 1, ('q', 'kv', 'o', 'g', 'u', 'd')))
        if layer == 0:
            pl.semaphore_wait(barrier, 3)
        wait(weight_loads(layer, ('o',)))
        sum_over_tp(2 * layer, lambda piece: matmul(att[...].astype(BF16), wo[layer, :, piece_columns(piece)]), residual, hid.at[2 * layer])
        residual = hid.at[2 * layer]
        normalize(residual, mgain_ref[...].astype(F32)[layer:layer + 1])
        wait(weight_loads(layer, ('g', 'u')))

        def mlp_step(i, carry):
            piece = piece_columns(i)
            gate = matmul(normed[...], wg[layer, :, piece])
            up = matmul(normed[...], wu[layer, :, piece])
            act[:, piece] = (gate / (1.0 + jnp.exp(-gate)) * up).astype(BF16)
            return carry

        lax.fori_loop(0, act.shape[1] // width, mlp_step, 0)
        wait(weight_loads(layer, ('d',)))
        target = out_ref if layer + 1 == layers else hid.at[2 * layer + 1]
        sum_over_tp(2 * layer + 1, lambda piece: matmul(act[...], wd[layer, :, piece_columns(piece)]), residual, target)
        residual = target


def run_layers(x, lengths, attn_gain, w_q, w_k, w_v, w_o, mlp_gain, w_gate, w_up, w_down, k_cache, v_cache, tp_size):
    rows, cols = x.shape
    layers = w_q.shape[0]
    head = k_cache.shape[-1]
    seqs, seq_len = k_cache.shape[1], k_cache.shape[3]
    dec = seqs - 1
    chunk = rows - dec
    heads = w_q.shape[2] // head
    inner = w_gate.shape[2]
    width = cols // tp_size
    sub = width // 2
    sums = 2 * layers
    freq = jnp.power(ROPE_BASE, -jnp.arange(0, head, 2, dtype=F32) / head)
    freq = jnp.broadcast_to(jnp.tile(freq, LANES // (head // 2))[None], (8, LANES))
    turned = lambda array: jnp.swapaxes(array, -1, -2)
    k_cols, v_cols = turned(k_cache)[:, :, 0], turned(v_cache)[:, :, 0]
    dma = pltpu.SemaphoreType.DMA
    vmem = pl.BlockSpec(memory_space=pltpu.VMEM)
    hbm = pl.BlockSpec(memory_space=pl.ANY)
    scratch = [
        ((layers, cols, heads * head), BF16), ((layers, 4 * head, cols), BF16), ((layers, heads * head, cols), BF16),
        ((layers, cols, inner), BF16), ((layers, cols, inner), BF16), ((layers, inner, cols), BF16),
        ((seqs, head, seq_len), BF16), ((seqs, head, seq_len), BF16),
        ((sums - 1, rows, cols), BF16), ((rows, cols), BF16), ((rows, inner), BF16), ((tp_size, rows, width), BF16),
        ((dec, LANES), jnp.int32), ((rows, LANES), F32), ((rows, LANES), F32),
        ((rows, heads * head), F32), ((rows, LANES), F32), ((rows, LANES), F32),
        ((heads, dec, LANES), F32), ((heads, dec, SEQS * head), F32), ((heads, chunk, LANES), BF16), ((heads, chunk, LANES), F32),
        ((rows, heads * head), F32),
        ((sums, 4, rows, width), BF16), ((sums, 4, rows, sub), BF16), ((sums, 6, rows, sub), BF16), ((sums, 2, rows, sub), BF16),
    ]
    semaphores = [(layers, 9), (layers, 2, dec // SEQS + 1), (sums, 4), (sums, 4), (sums, 6), (sums, 6), (sums, 6), (sums, 6), (sums, 7), (sums, 7)]
    return pl.pallas_call(
        functools.partial(layer_kernel, tp_size // 2),
        out_shape=jax.ShapeDtypeStruct(x.shape, x.dtype),
        in_specs=[vmem, pl.BlockSpec(memory_space=pltpu.SMEM), vmem, vmem, vmem] + [hbm] * 9,
        out_specs=vmem,
        scratch_shapes=[pltpu.VMEM(shape, dtype) for shape, dtype in scratch] + [dma(shape) for shape in semaphores],
        compiler_params=pltpu.CompilerParams(collective_id=0, has_side_effects=True, vmem_limit_bytes=VMEM_LIMIT),
    )(x, lengths, freq, attn_gain, mlp_gain, w_q, turned(w_k), turned(w_v), w_o, w_gate, w_up, w_down, k_cols, v_cols)


def solution(mesh):
    col_spec = P(None, None, 'tp')
    row_spec = P(None, 'tp', None)
    cache_spec = P(None, 'dp', 'tp', None, None)
    in_specs = (P('dp', None), P('dp'), P(), col_spec, col_spec, col_spec, row_spec, P(), col_spec, col_spec, row_spec, cache_spec, cache_spec)
    body = functools.partial(run_layers, tp_size=mesh.shape['tp'])
    return jax.shard_map(body, mesh=mesh, in_specs=in_specs, out_specs=P('dp', None), check_vma=False)
```

time: 335 us -> 115 us (0.34)
  waiting for transfers between devices: 222 us -> 0 us
  Pallas kernels: 0 us -> 112 us
  matrix products: 53.9 us -> 0 us
  other arithmetic: 29.5 us -> 0.01 us
  between operations: 13.7 us -> 0.01 us
  local copies, waits for them, and re-layouts: 13.5 us -> 2.78 us
    psum x4 -> x0, waiting for transfers between devices: 222 us -> none  [the longest x2 112 us: decoder_layer(): attn_sum = lax.psum(attn_part, 'tp')]
    pallas_call x0 -> x1, Pallas kernels: none -> 112 us  [run_layers(): pl.pallas_call(functools.partial(layer_kernel, tp_size // 2), out_shape=j...]
    dot_general x26 -> x0, matrix products: 53.9 us -> none  [the longest x2 12.6 us: decoder_layer(): jnp.dot(activated, w_down, preferred_element_type=jnp.float32)]
    reduce_sum x8 -> x0, other arithmetic: 11 us -> none  [the longest x4 6.03 us: rms_norm(): jnp.mean(x_f32 * x_f32, axis=-1, keepdims=True) + EPSILON]
    convert_element_type x9 -> x0, other arithmetic: 7.96 us -> none  [the longest x2 3.66 us: attention(): jax.nn.softmax(jnp.concatenate([dec_cache, dec_self], axis=-1), axis=-1)]
    concatenate x4 -> x0, other arithmetic: 6.01 us -> none  [the longest x2 5.47 us: attention(): jnp.concatenate([dec_cache, dec_self], axis=-1)]
    another operation x6 -> x1, local copies, waits for them, and re-layouts: 5.28 us -> 0.01 us  [run_layers(): jnp.tile(freq, LANES // (head // 2))[None]]
    dot_general x2 -> x0, local copies, waits for them, and re-layouts: 3.83 us -> none  [attention(): jnp.einsum('bgrd,bgsd->bgrs', q_dec, k_cache[:dec_rows], preferred_elemen...]
  transfers between devices with their start and end apart: 4 -> 0, of which waited for: 4 -> 0; matrix products, arithmetic and copies ran while one was open for 0% -> 0% of each run, Pallas kernels for 0% -> 0%
where the time goes in v2:
time: 115 us
  Pallas kernels  112 us (97%)
  local copies, waits for them, and re-layouts  2.78 us (2%)
    pallas_call x1, Pallas kernels, run_layers(): pl.pallas_call(functools.partial(layer_kernel, tp_size // 2), out_shape=j...  112 us

profile of v2, /device:TPU:81, one launch (start us, length us, event | category | flops | bytes accessed | tf_op | source)
XLA Modules:
  0.0 114.6 jit_solution(13473951225515736824)
XLA Ops:
  0.0 0.1 broadcast_in_dim.7
  0.1 0.6 broadcast_in_dim.8.freq_ref
  0.7 111.8 %shard_map.127 = bf16[192,2048]{1,0:T(8,128)(2,1)} custom-call(bf16[192,2048]{1,0:T(8,128)(2,1)} %x_ref.1, s32[65]{0:T(128)} %lens_ref.1, f32[8,128]{1,0:T(8,128)} %broadcast_in_dim.8.freq_ref, bf16[2,2048]{1,0:T(2,128)(2,1)} %again_ref.1, bf16[2,2048]{1,0:T(2,128)(2,1)} %mgain_ref.1, bf16[2,2048,256]{2,1,0:T(8,128)(2,1)} %wq_hbm.1, ...), custom_call_target="tpu_custom_call" | custom-call | tf_op jit(solution)/shard_map/pallas_call | solution.py:419
  112.5 2.1 %copy.17 = bf16[192,2048]{1,0:T(8,128)(2,1)} copy(bf16[192,2048]{1,0:T(8,128)(2,1)} %shard_map.127) | data formatting | bytes 1572864
  (2 shorter events, 0.0 us)

commit v3 on v2

v3 whole, which is shorter than its diff:
```python
import functools

import jax
import jax.numpy as jnp
from jax import lax
from jax.experimental import pallas as pl
from jax.experimental.pallas import tpu as pltpu
from jax.sharding import PartitionSpec as P

ROPE_BASE = 500000.0
EPSILON = 1e-5
MESH = pl.DeviceIdType.MESH
LANES = 128
SEQS = 8
CACHE_LOADS = 4
NEAR_WAIT, NEAR_WIRE, FAR_WAIT, FAR_WIRE = 2.6, 2.1, 3.4, 4.2
VMEM_LIMIT = 67043328
F32 = jnp.float32
BF16 = jnp.bfloat16
NT = (((1,), (1,)), ((), ()))


def matmul(a, b):
    return jnp.dot(a, b, preferred_element_type=F32)


def matmul_nt(a, b):
    return lax.dot_general(a, b, NT, preferred_element_type=F32)


def run_streams(streams):
    now, ready = 0.0, [0.0] * len(streams)
    live = set(range(len(streams)))
    while live:
        pick = min(sorted(live), key=lambda i: ready[i])
        now = max(now, ready[pick])
        try:
            busy, wait = next(streams[pick])
        except StopIteration:
            live.discard(pick)
            continue
        now += busy
        ready[pick] = now + wait


def layer_kernel(chips, x_ref, lens_ref, freq_ref, again_ref, mgain_ref, wq_hbm, wk_hbm, wv_hbm, wo_hbm, wg_hbm, wu_hbm, wd_hbm, k_hbm, v_hbm,
                 out_ref,
                 wq, wkv, wo, wg, wu, wd, kbuf, vbuf, hid, normed, act, lens_v, cos_t, sin_t, q_t, k_t, v_t, self_t, qbd, qh, oh, att,
                 part_a, pair_in_a, pair_sum_a, ring_in_a, part_b, pair_in_b, pair_sum_b, ring_in_b,
                 load_sem, cache_sem, pair_send, pair_recv, ring_send, ring_recv, gather_send, gather_recv, share_send, share_recv):
    layers = wq.shape[0]
    rows, cols = x_ref.shape
    dec = lens_v.shape[0]
    chunk = rows - dec
    head = k_hbm.shape[2]
    seq_len = k_hbm.shape[3]
    heads = qbd.shape[0]
    scale = head ** -0.5
    loads = cache_sem.shape[2] - 1
    load_seqs = dec // loads
    half = cols // 2
    width = half // chips
    span = (slice(0, dec), slice(dec, rows))
    parts = (part_a, part_b)
    buffers = ((pair_in_a, pair_sum_a, ring_in_a), (pair_in_b, pair_sum_b, ring_in_b))

    me = lax.axis_index('tp')
    core, chip = lax.rem(me, 2), lax.div(me, 2)

    def at_chip(step):
        return lax.rem(chip + step + chips, chips)

    partner = {'tp': chip * 2 + 1 - core}
    right = {'tp': at_chip(1) * 2 + core}
    left = {'tp': at_chip(-1) * 2 + core}
    far = {'tp': at_chip(2) * 2 + core}
    others = (far, right, left)

    def load(layer, name):
        src, dst, slot = {
            'q': (wq_hbm.at[layer], wq.at[layer], 0),
            'k0': (wk_hbm.at[layer], wkv.at[layer, 0:head], 1),
            'k1': (wk_hbm.at[layer], wkv.at[layer, head:2 * head], 2),
            'v0': (wv_hbm.at[layer], wkv.at[layer, 2 * head:3 * head], 3),
            'v1': (wv_hbm.at[layer], wkv.at[layer, 3 * head:4 * head], 4),
            'o': (wo_hbm.at[layer], wo.at[layer], 5),
            'g': (wg_hbm.at[layer], wg.at[layer], 6),
            'u': (wu_hbm.at[layer], wu.at[layer], 7),
            'd': (wd_hbm.at[layer], wd.at[layer], 8),
        }[name]
        return pltpu.make_async_copy(src, dst, load_sem.at[layer, slot])

    def cache_load(layer, which, index):
        src, dst = ((k_hbm, kbuf), (v_hbm, vbuf))[which]
        block = pl.ds(index * load_seqs, load_seqs) if index < loads else dec
        return pltpu.make_async_copy(src.at[layer, block], dst.at[block], cache_sem.at[layer, which, index])

    landed = set()

    def arrive(layer, names):
        for name in names:
            if (layer, name) not in landed:
                landed.add((layer, name))
                load(layer, name).wait()

    def arrive_cache(layer, index):
        for which in range(2):
            cache_load(layer, which, index).wait()

    def start(layer, names):
        for name in names:
            load(layer, name).start()

    def start_cache(layer, indices):
        for index in indices:
            for which in range(2):
                cache_load(layer, which, index).start()

    projections = ('q', 'k0', 'k1', 'v0', 'v1')
    start(0, projections)
    start_cache(0, [loads])
    start(0, ('o',))
    start_cache(0, range(loads))
    start(0, ('g', 'u', 'd'))

    barrier = pltpu.get_barrier_semaphore()
    for device in (partner, right, left, far):
        pl.semaphore_signal(barrier, inc=1, device_id=device, device_id_type=MESH)

    def fill(row, carry):
        lens_v[pl.ds(row, 1), :] = jnp.full((1, LANES), lens_ref[row], jnp.int32)
        return carry

    lax.fori_loop(0, dec, fill, 0)

    def table(row, positions):
        angles = positions.astype(F32) * freq_ref[0:1, :]
        cos_t[pl.ds(row, 8), :] = jnp.cos(angles)
        sin_t[pl.ds(row, 8), :] = jnp.sin(angles)

    def dec_table(i, carry):
        row = pl.multiple_of(i * 8, 8)
        table(row, lens_v[pl.ds(row, 8), :])
        return carry

    def chunk_table(i, carry):
        row = pl.multiple_of(i * 8, 8)
        table(dec + row, lens_ref[dec] + row + lax.broadcasted_iota(jnp.int32, (8, LANES), 0))
        return carry

    lax.fori_loop(0, dec // 8, dec_table, 0)
    lax.fori_loop(0, chunk // 8, chunk_table, 0)

    def normalize(stream, src, gain):
        first, last = span[stream].start, span[stream].stop

        def block(i, carry):
            band = pl.ds(pl.multiple_of(first + i * 16, 16), 16)
            values = src[band, :].astype(F32)
            inv = lax.rsqrt(jnp.sum(values * values, axis=1, keepdims=True) * (1.0 / cols) + EPSILON)
            normed[band, :] = (values * inv * gain).astype(BF16)
            return carry

        lax.fori_loop(0, (last - first) // 16, block, 0, unroll=4)

    def rope(stream, values):
        wide = values.shape[1]
        lane = lax.broadcasted_iota(jnp.int32, values.shape, 1)
        turned = jnp.where(lane % head < head // 2, -pltpu.roll(values, wide - head // 2, 1), pltpu.roll(values, head // 2, 1))
        cos, sin = cos_t[span[stream], :], sin_t[span[stream], :]
        if wide > LANES:
            cos, sin = jnp.concatenate([cos, cos], axis=1), jnp.concatenate([sin, sin], axis=1)
        return (values * cos + turned * sin).astype(BF16).astype(F32)

    def project(stream, layer):
        values = normed[span[stream], :]
        q_t[span[stream], :] = rope(stream, matmul(values, wq[layer]).astype(BF16).astype(F32))
        kv = matmul_nt(values, wkv[layer]).astype(BF16)
        k_t[span[stream], :] = rope(stream, kv[:, :LANES].astype(F32))
        v_t[span[stream], :] = kv[:, LANES:].astype(F32)

    def decode_setup():
        lane = lax.broadcasted_iota(jnp.int32, (dec, LANES), 1)
        keys = k_t[0:dec, :]
        for pair in range(heads // 2):
            block = q_t[0:dec, pair * LANES:(pair + 1) * LANES]
            swapped = pltpu.roll(block, head, 1)
            product = block * keys
            for side in range(2):
                r = 2 * pair + side
                mine = (lane < head) if side == 0 else (lane >= head)
                self_t[r] = jnp.broadcast_to(jnp.sum(jnp.where(mine, product, 0.0), axis=1, keepdims=True) * scale, (dec, LANES))
                twice = jnp.where(mine, block, swapped)
                wide = jnp.concatenate([twice] * (SEQS * head // LANES), axis=1)
                col = lax.broadcasted_iota(jnp.int32, wide.shape, 1)
                row = lax.broadcasted_iota(jnp.int32, wide.shape, 0)
                qbd[r] = jnp.where(col // head == row % SEQS, wide, 0.0)

    def decode(bands):
        probs, own_probs = [], []
        for first in bands:
            band = slice(first, first + SEQS)
            queries = qbd[:, band, :].reshape(heads * SEQS, SEQS * head).astype(BF16)
            logits = matmul(queries, kbuf[band].reshape(SEQS * head, seq_len)) * scale
            logits = logits.reshape(heads, SEQS, seq_len)
            seen = lax.broadcasted_iota(jnp.int32, (SEQS, seq_len), 1) < lens_v[band, 0:1]
            logits = jnp.where(seen[None], logits, -jnp.inf)
            own = self_t[:, band, 0:1]
            top = jnp.maximum(jnp.max(logits, axis=2, keepdims=True), own)
            weights = jnp.exp(logits - top)
            own_weight = jnp.exp(own - top)
            inv = 1.0 / (jnp.sum(weights, axis=2, keepdims=True) + own_weight)
            probs.append((weights * inv).astype(BF16).reshape(heads * SEQS, seq_len))
            own_probs.append((own_weight * inv).astype(BF16).astype(F32))
        for first, prob, own_prob in zip(bands, probs, own_probs):
            band = slice(first, first + SEQS)
            mixed = matmul_nt(prob, vbuf[band].reshape(SEQS * head, seq_len))
            col = lax.broadcasted_iota(jnp.int32, mixed.shape, 1)
            row = lax.broadcasted_iota(jnp.int32, mixed.shape, 0)
            mixed = jnp.where(col // head == row % SEQS, mixed, 0.0)
            folded = mixed[:, 0:LANES]
            for i in range(1, SEQS * head // LANES):
                folded = folded + mixed[:, i * LANES:(i + 1) * LANES]
            folded = folded + pltpu.roll(folded, head, 1)
            result = folded.reshape(heads, SEQS, LANES) + own_prob * v_t[band, :][None]
            lane = lax.broadcasted_iota(jnp.int32, (SEQS, LANES), 1)
            att[band, 0:LANES] = jnp.where(lane < head, result[0], result[1])
            att[band, LANES:2 * LANES] = jnp.where(lane < head, result[2], result[3])

    def prefill_setup():
        lane = lax.broadcasted_iota(jnp.int32, (chunk, LANES), 1)
        for pair in range(heads // 2):
            block = q_t[dec:rows, pair * LANES:(pair + 1) * LANES]
            qh[2 * pair] = jnp.where(lane < head, block, 0.0).astype(BF16)
            qh[2 * pair + 1] = jnp.where(lane >= head, block, 0.0).astype(BF16)

    def prefill(r):
        queries = qh[r]
        keys = kbuf[dec]
        logits = matmul(queries, jnp.concatenate([keys, keys], axis=0)) * scale
        seen = lax.broadcasted_iota(jnp.int32, (chunk, seq_len), 1) < lens_ref[dec]
        logits = jnp.where(seen, logits, -jnp.inf)
        own = matmul_nt(queries, k_t[dec:rows, :].astype(BF16)) * scale
        causal = lax.broadcasted_iota(jnp.int32, (chunk, chunk), 1) <= lax.broadcasted_iota(jnp.int32, (chunk, chunk), 0)
        own = jnp.where(causal, own, -jnp.inf)
        top = jnp.maximum(jnp.max(logits, axis=1, keepdims=True), jnp.max(own, axis=1, keepdims=True))
        weights = jnp.exp(logits - top)
        own_weights = jnp.exp(own - top)
        inv = 1.0 / (jnp.sum(weights, axis=1, keepdims=True) + jnp.sum(own_weights, axis=1, keepdims=True))
        probs = (weights * inv).astype(BF16)
        own_probs = (own_weights * inv).astype(BF16)
        values = vbuf[dec]
        oh[r] = matmul_nt(probs, jnp.concatenate([values, values], axis=0)) + matmul(own_probs, v_t[dec:rows, :].astype(BF16))

    def prefill_end():
        lane = lax.broadcasted_iota(jnp.int32, (chunk, LANES), 1)
        for pair in range(heads // 2):
            att[dec:rows, pair * LANES:(pair + 1) * LANES] = jnp.where(lane < head, oh[2 * pair], oh[2 * pair + 1])

    def copy(src, dst, send, recv, to):
        return pltpu.make_async_remote_copy(src_ref=src, dst_ref=dst, send_sem=send, recv_sem=recv, device_id=to, device_id_type=MESH)

    def step_of(slot):
        high, low = slot // 2, slot % 2
        return 2 - low + high * (1 - 2 * low)

    greeted = []

    def sum_over_tp(stream, index, product, product_time, base, target):
        part = parts[stream]
        pair_in, pair_sum, ring_in = buffers[stream]
        band = span[stream]
        sems = index * 2 + stream
        scale_wire = (band.stop - band.start) / rows

        def piece_of(which_core, slot):
            return which_core * chips + at_chip(step_of(slot))

        def pair_copy(slot):
            return copy(part.at[piece_of(1 - core, slot)], pair_in.at[index, slot], pair_send.at[sems, slot], pair_recv.at[sems, slot], partner)

        def theirs(slot):
            piece = piece_of(1 - core, slot)
            part[piece] = product(piece).astype(BF16)

        def ours(slot):
            piece = piece_of(core, slot)
            part[piece] = product(piece).astype(BF16)

        if not greeted:
            greeted.append(True)
            pl.semaphore_wait(barrier, 4)
        for slot in range(4):
            theirs(slot)
        for slot in range(4):
            pair_copy(slot).start()
        for slot in range(4):
            ours(slot)
        yield product_time, 1.1 + 0.3 * scale_wire

        def columns(which_core, which_chip):
            return pl.ds(pl.multiple_of(which_core * half + which_chip * width, LANES), width)

        def pair_add(slot):
            return part[piece_of(core, slot)].astype(F32) + pair_in[index, slot].astype(F32)

        def scatter(slot):
            return copy(pair_sum.at[index, slot], ring_in.at[index, slot], ring_send.at[sems, slot], ring_recv.at[sems, slot], others[slot])

        def gather(slot):
            block = target.at[band, columns(core, chip)]
            return copy(block, block, gather_send.at[sems, slot], gather_recv.at[sems, slot], others[slot])

        def share(step, slot):
            block = target.at[band, columns(core, at_chip(step))]
            return copy(block, block, share_send.at[sems, slot], share_recv.at[sems, slot], partner)

        for slot in range(3):
            pair_copy(slot).wait_recv()
            pair_sum[index, slot] = pair_add(slot).astype(BF16)
            scatter(slot).start()
        yield 0.25, FAR_WAIT + FAR_WIRE * scale_wire
        pair_copy(3).wait_recv()
        total = pair_add(3) + base[band, columns(core, chip)].astype(F32)
        for slot in (1, 2, 0):
            scatter(slot).wait_recv()
            total = total + ring_in[index, slot].astype(F32)
        target[band, columns(core, chip)] = total.astype(BF16)
        for slot in range(3):
            gather(slot).start()
        share(0, 3).start()
        yield 0.25, NEAR_WAIT + NEAR_WIRE * scale_wire
        for slot, step in ((1, -1), (2, 1)):
            gather(slot).wait_recv()
            share(step, slot).start()
        yield 0.05, FAR_WAIT - NEAR_WAIT + (FAR_WIRE - NEAR_WIRE) * scale_wire
        gather(0).wait_recv()
        share(2, 0).start()
        yield 0.05, 1.0 + 0.2 * scale_wire
        for slot in range(4):
            share(0, slot).wait_recv()
        for slot in range(4):
            pair_copy(slot).wait_send()
            share(0, slot).wait_send()
        for slot in range(3):
            scatter(slot).wait_send()
            gather(slot).wait_send()

    def piece_columns(piece):
        return pl.ds(pl.multiple_of(piece * width, LANES), width)

    attended = [0] * layers

    def attention_done(layer):
        attended[layer] += 1
        if attended[layer] == 2 and layer + 1 < layers:
            start(layer + 1, projections)
            start_cache(layer + 1, [loads])
            start(layer + 1, ('o',))
            start_cache(layer + 1, range(loads))
            start(layer + 1, ('g', 'u', 'd'))

    def stream_steps(stream):
        band = span[stream]
        residual = x_ref
        for layer in range(layers):
            normalize(stream, residual, again_ref[...].astype(F32)[layer:layer + 1])
            yield 0.3, 0.0
            arrive(layer, projections)
            project(stream, layer)
            if stream == 0:
                decode_setup()
                yield 1.0, 0.0
                for index in range(loads):
                    arrive_cache(layer, index)
                    decode(range(index * load_seqs, (index + 1) * load_seqs, SEQS))
                    yield 1.4, 0.0
            else:
                prefill_setup()
                yield 0.8, 0.0
                arrive_cache(layer, loads)
                for r in range(heads):
                    prefill(r)
                    yield 0.55, 0.0
                prefill_end()
            attention_done(layer)
            arrive(layer, ('o',))
            target = hid.at[2 * layer]
            yield from sum_over_tp(stream, 2 * layer, lambda piece: matmul(att[band, :].astype(BF16), wo[layer, :, piece_columns(piece)]), 0.3, residual, target)
            residual = target
            normalize(stream, residual, mgain_ref[...].astype(F32)[layer:layer + 1])
            arrive(layer, ('g', 'u'))

            def mlp_step(i, carry):
                piece = piece_columns(i)
                gate = matmul(normed[band, :], wg[layer, :, piece])
                up = matmul(normed[band, :], wu[layer, :, piece])
                act[band, piece] = (gate / (1.0 + jnp.exp(-gate)) * up).astype(BF16)
                return carry

            lax.fori_loop(0, act.shape[1] // width, mlp_step, 0, unroll=2)
            yield 1.4, 0.0
            arrive(layer, ('d',))
            target = out_ref if layer + 1 == layers else hid.at[2 * layer + 1]
            yield from sum_over_tp(stream, 2 * layer + 1, lambda piece: matmul(act[band, :], wd[layer, :, piece_columns(piece)]), 0.6, residual, target)
            residual = target

    run_streams([stream_steps(1), stream_steps(0)])


def run_layers(x, lengths, attn_gain, w_q, w_k, w_v, w_o, mlp_gain, w_gate, w_up, w_down, k_cache, v_cache, tp_size):
    rows, cols = x.shape
    layers = w_q.shape[0]
    head = k_cache.shape[-1]
    seqs, seq_len = k_cache.shape[1], k_cache.shape[3]
    dec = seqs - 1
    chunk = rows - dec
    heads = w_q.shape[2] // head
    inner = w_gate.shape[2]
    width = cols // tp_size
    sums = 2 * layers
    freq = jnp.power(ROPE_BASE, -jnp.arange(0, head, 2, dtype=F32) / head)
    freq = jnp.broadcast_to(jnp.tile(freq, LANES // (head // 2))[None], (8, LANES))
    turned = lambda array: jnp.swapaxes(array, -1, -2)
    k_cols, v_cols = turned(k_cache)[:, :, 0], turned(v_cache)[:, :, 0]
    dma = pltpu.SemaphoreType.DMA
    vmem = pl.BlockSpec(memory_space=pltpu.VMEM)
    hbm = pl.BlockSpec(memory_space=pl.ANY)
    scratch = [
        ((layers, cols, heads * head), BF16), ((layers, 4 * head, cols), BF16), ((layers, heads * head, cols), BF16),
        ((layers, cols, inner), BF16), ((layers, cols, inner), BF16), ((layers, inner, cols), BF16),
        ((seqs, head, seq_len), BF16), ((seqs, head, seq_len), BF16),
        ((sums - 1, rows, cols), BF16), ((rows, cols), BF16), ((rows, inner), BF16),
        ((dec, LANES), jnp.int32), ((rows, LANES), F32), ((rows, LANES), F32),
        ((rows, heads * head), F32), ((rows, LANES), F32), ((rows, LANES), F32),
        ((heads, dec, LANES), F32), ((heads, dec, SEQS * head), F32), ((heads, chunk, LANES), BF16), ((heads, chunk, LANES), F32),
        ((rows, heads * head), F32),
    ]
    for band in (dec, chunk):
        scratch += [((tp_size, band, width), BF16), ((sums, 4, band, width), BF16), ((sums, 3, band, width), BF16), ((sums, 3, band, width), BF16)]
    semaphores = [(layers, 9), (layers, 2, CACHE_LOADS + 1)] + [(2 * sums, count) for count in (4, 4, 3, 3, 3, 3, 4, 4)]
    return pl.pallas_call(
        functools.partial(layer_kernel, tp_size // 2),
        out_shape=jax.ShapeDtypeStruct(x.shape, x.dtype),
        in_specs=[vmem, pl.BlockSpec(memory_space=pltpu.SMEM), vmem, vmem, vmem] + [hbm] * 9,
        out_specs=vmem,
        scratch_shapes=[pltpu.VMEM(shape, dtype) for shape, dtype in scratch] + [dma(shape) for shape in semaphores],
        compiler_params=pltpu.CompilerParams(collective_id=0, has_side_effects=True, vmem_limit_bytes=VMEM_LIMIT),
    )(x, lengths, freq, attn_gain, mlp_gain, w_q, turned(w_k), turned(w_v), w_o, w_gate, w_up, w_down, k_cols, v_cols)


def solution(mesh):
    col_spec = P(None, None, 'tp')
    row_spec = P(None, 'tp', None)
    cache_spec = P(None, 'dp', 'tp', None, None)
    in_specs = (P('dp', None), P('dp'), P(), col_spec, col_spec, col_spec, row_spec, P(), col_spec, col_spec, row_spec, cache_spec, cache_spec)
    body = functools.partial(run_layers, tp_size=mesh.shape['tp'])
    return jax.shard_map(body, mesh=mesh, in_specs=in_specs, out_specs=P('dp', None), check_vma=False)
```

time: 115 us -> 98.2 us (0.85)
  Pallas kernels: 112 us -> 95.3 us
    pallas_call x1, Pallas kernels: 112 us -> 95.3 us  [run_layers(): pl.pallas_call(functools.partial(layer_kernel, tp_size // 2), out_shape=j...]
where the time goes in v3:
time: 98.2 us; the launch traced here: 98.1 us
  Pallas kernels  95.3 us (97%)
  local copies, waits for them, and re-layouts  2.78 us (3%)
    pallas_call x1, Pallas kernels, run_layers(): pl.pallas_call(functools.partial(layer_kernel, tp_size // 2), out_shape=j...  95.3 us
    unnamed x1, local copies, waits for them, and re-layouts  2.09 us

profile of v3, /device:TPU:81, one launch (start us, length us, event | category | flops | bytes accessed | tf_op | source)
XLA Modules:
  0.0 98.1 jit_solution(15758834574085178455)
XLA Ops:
  0.0 0.1 broadcast_in_dim.7
  0.1 0.6 broadcast_in_dim.8.freq_ref
  0.7 95.3 %shard_map.127 = bf16[192,2048]{1,0:T(8,128)(2,1)} custom-call(bf16[192,2048]{1,0:T(8,128)(2,1)} %x_ref.1, s32[65]{0:T(128)} %lens_ref.1, f32[8,128]{1,0:T(8,128)} %broadcast_in_dim.8.freq_ref, bf16[2,2048]{1,0:T(2,128)(2,1)} %again_ref.1, bf16[2,2048]{1,0:T(2,128)(2,1)} %mgain_ref.1, bf16[2,2048,256]{2,1,0:T(8,128)(2,1)} %wq_hbm.1, ...), custom_call_target="tpu_custom_call" | custom-call | tf_op jit(solution)/shard_map/pallas_call | solution.py:442
  96.0 2.1 %copy.17 = bf16[192,2048]{1,0:T(8,128)(2,1)} copy(bf16[192,2048]{1,0:T(8,128)(2,1)} %shard_map.127) | data formatting | bytes 1572864
  (2 shorter events, 0.0 us)

commit v4 on v3

--- a/solution.py
+++ b/solution.py
@@ -30,9 +30,14 @@
 
 def run_streams(streams):
     now, ready = 0.0, [0.0] * len(streams)
+    arrived = [False] * len(streams)
     live = set(range(len(streams)))
+
+    def order(i):
+        return (0, 0, ready[i]) if ready[i] <= now and arrived[i] else (0, 1, i) if ready[i] <= now else (1, ready[i], i)
+
     while live:
-        pick = min(sorted(live), key=lambda i: ready[i])
+        pick = min(sorted(live), key=order)
         now = max(now, ready[pick])
         try:
             busy, wait = next(streams[pick])
@@ -41,6 +46,7 @@
             continue
         now += busy
         ready[pick] = now + wait
+        arrived[pick] = wait > 0
 
 
 def layer_kernel(chips, x_ref, lens_ref, freq_ref, again_ref, mgain_ref, wq_hbm, wk_hbm, wv_hbm, wo_hbm, wg_hbm, wu_hbm, wd_hbm, k_hbm, v_hbm,
@@ -120,8 +126,6 @@
     start(0, projections)
     start_cache(0, [loads])
     start(0, ('o',))
-    start_cache(0, range(loads))
-    start(0, ('g', 'u', 'd'))
 
     barrier = pltpu.get_barrier_semaphore()
     for device in (partner, right, left, far):
@@ -367,6 +371,8 @@
             normalize(stream, residual, again_ref[...].astype(F32)[layer:layer + 1])
             yield 0.3, 0.0
             arrive(layer, projections)
+            if layer == 0 and stream == 1:
+                start_cache(0, range(loads))
             project(stream, layer)
             if stream == 0:
                 decode_setup()
@@ -383,6 +389,8 @@
                     prefill(r)
                     yield 0.55, 0.0
                 prefill_end()
+                if layer == 0:
+                    start(layer, ('g', 'u', 'd'))
             attention_done(layer)
             arrive(layer, ('o',))
             target = hid.at[2 * layer]

time: 98.2 us -> 86.1 us (0.88)
  Pallas kernels: 95.3 us -> 83.1 us
    pallas_call x1, Pallas kernels: 95.3 us -> 83.1 us  [run_layers(): pl.pallas_call(functools.partial(layer_kernel, tp_size // 2), out_shape=j...]
where the time goes in v4:
time: 86.1 us; the launch traced here: 85.9 us
  Pallas kernels  83.1 us (97%)
  local copies, waits for them, and re-layouts  2.78 us (3%)
    pallas_call x1, Pallas kernels, run_layers(): pl.pallas_call(functools.partial(layer_kernel, tp_size // 2), out_shape=j...  83.1 us
    unnamed x1, local copies, waits for them, and re-layouts  2.09 us

profile of v4, /device:TPU:81, one launch (start us, length us, event | category | flops | bytes accessed | tf_op | source)
XLA Modules:
  0.0 85.9 jit_solution(8314771164717934086)
XLA Ops:
  0.0 0.1 broadcast_in_dim.7
  0.1 0.6 broadcast_in_dim.8.freq_ref
  0.7 83.1 %shard_map.127 = bf16[192,2048]{1,0:T(8,128)(2,1)} custom-call(bf16[192,2048]{1,0:T(8,128)(2,1)} %x_ref.1, s32[65]{0:T(128)} %lens_ref.1, f32[8,128]{1,0:T(8,128)} %broadcast_in_dim.8.freq_ref, bf16[2,2048]{1,0:T(2,128)(2,1)} %again_ref.1, bf16[2,2048]{1,0:T(2,128)(2,1)} %mgain_ref.1, bf16[2,2048,256]{2,1,0:T(8,128)(2,1)} %wq_hbm.1, ...), custom_call_target="tpu_custom_call" | custom-call | tf_op jit(solution)/shard_map/pallas_call | solution.py:450
  83.9 2.1 %copy.17 = bf16[192,2048]{1,0:T(8,128)(2,1)} copy(bf16[192,2048]{1,0:T(8,128)(2,1)} %shard_map.127) | data formatting | bytes 1572864
  (2 shorter events, 0.0 us)

commit v5 on v4

--- a/solution.py
+++ b/solution.py
@@ -1,4 +1,5 @@
 import functools
+import math
 
 import jax
 import jax.numpy as jnp
@@ -13,7 +14,7 @@
 LANES = 128
 SEQS = 8
 CACHE_LOADS = 4
-NEAR_WAIT, NEAR_WIRE, FAR_WAIT, FAR_WIRE = 2.6, 2.1, 3.4, 4.2
+NEAR_WAIT, NEAR_WIRE, FAR_WAIT, FAR_WIRE = 2.4, 1.4, 3.0, 2.8
 VMEM_LIMIT = 67043328
 F32 = jnp.float32
 BF16 = jnp.bfloat16
@@ -49,13 +50,13 @@
         arrived[pick] = wait > 0
 
 
-def layer_kernel(chips, x_ref, lens_ref, freq_ref, again_ref, mgain_ref, wq_hbm, wk_hbm, wv_hbm, wo_hbm, wg_hbm, wu_hbm, wd_hbm, k_hbm, v_hbm,
+def layer_kernel(chips, x_hbm, lens_ref, again_ref, mgain_ref, wq_hbm, wk_hbm, wv_hbm, wo_hbm, wg_hbm, wu_hbm, wd_hbm, k_hbm, v_hbm,
                  out_ref,
-                 wq, wkv, wo, wg, wu, wd, kbuf, vbuf, hid, normed, act, lens_v, cos_t, sin_t, q_t, k_t, v_t, self_t, qbd, qh, oh, att,
+                 x_ref, wq, wkv, wo, wg, wu, wd, kbuf, vbuf, hid, normed, act, lens_v, cos_t, sin_t, q_t, k_t, v_t, self_t, qbd, qh, oh, att,
                  part_a, pair_in_a, pair_sum_a, ring_in_a, part_b, pair_in_b, pair_sum_b, ring_in_b,
-                 load_sem, cache_sem, pair_send, pair_recv, ring_send, ring_recv, gather_send, gather_recv, share_send, share_recv):
+                 io_sem, load_sem, cache_sem, pair_send, pair_recv, ring_send, ring_recv, gather_send, gather_recv, share_send, share_recv):
     layers = wq.shape[0]
-    rows, cols = x_ref.shape
+    rows, cols = x_hbm.shape
     dec = lens_v.shape[0]
     chunk = rows - dec
     head = k_hbm.shape[2]
@@ -123,7 +124,10 @@
                 cache_load(layer, which, index).start()
 
     projections = ('q', 'k0', 'k1', 'v0', 'v1')
+    x_loads = [pltpu.make_async_copy(x_hbm.at[band], x_ref.at[band], io_sem.at[side]) for side, band in enumerate(span)]
+    x_loads[1].start()
     start(0, projections)
+    x_loads[0].start()
     start_cache(0, [loads])
     start(0, ('o',))
 
@@ -137,8 +141,11 @@
 
     lax.fori_loop(0, dec, fill, 0)
 
+    pair_ids = (lax.broadcasted_iota(jnp.int32, (8, LANES), 1) % (head // 2)).astype(F32)
+    freq = jnp.exp(pair_ids * (-2.0 * math.log(ROPE_BASE) / head))
+
     def table(row, positions):
-        angles = positions.astype(F32) * freq_ref[0:1, :]
+        angles = positions.astype(F32) * freq
         cos_t[pl.ds(row, 8), :] = jnp.cos(angles)
         sin_t[pl.ds(row, 8), :] = jnp.sin(angles)
 
@@ -367,6 +374,7 @@
     def stream_steps(stream):
         band = span[stream]
         residual = x_ref
+        x_loads[stream].wait()
         for layer in range(layers):
             normalize(stream, residual, again_ref[...].astype(F32)[layer:layer + 1])
             yield 0.3, 0.0
@@ -406,14 +414,19 @@
                 act[band, piece] = (gate / (1.0 + jnp.exp(-gate)) * up).astype(BF16)
                 return carry
 
-            lax.fori_loop(0, act.shape[1] // width, mlp_step, 0, unroll=2)
+            lax.fori_loop(0, act.shape[1] // width, mlp_step, 0, unroll=4)
             yield 1.4, 0.0
             arrive(layer, ('d',))
-            target = out_ref if layer + 1 == layers else hid.at[2 * layer + 1]
+            target = hid.at[2 * layer + 1]
             yield from sum_over_tp(stream, 2 * layer + 1, lambda piece: matmul(act[band, :], wd[layer, :, piece_columns(piece)]), 0.6, residual, target)
             residual = target
-
+        stores.append(pltpu.make_async_copy(residual.at[band], out_ref.at[band], io_sem.at[2 + stream]))
+        stores[-1].start()
+
+    stores = []
     run_streams([stream_steps(1), stream_steps(0)])
+    for each in stores:
+        each.wait()
 
 
 def run_layers(x, lengths, attn_gain, w_q, w_k, w_v, w_o, mlp_gain, w_gate, w_up, w_down, k_cache, v_cache, tp_size):
@@ -427,18 +440,17 @@
     inner = w_gate.shape[2]
     width = cols // tp_size
     sums = 2 * layers
-    freq = jnp.power(ROPE_BASE, -jnp.arange(0, head, 2, dtype=F32) / head)
-    freq = jnp.broadcast_to(jnp.tile(freq, LANES // (head // 2))[None], (8, LANES))
     turned = lambda array: jnp.swapaxes(array, -1, -2)
     k_cols, v_cols = turned(k_cache)[:, :, 0], turned(v_cache)[:, :, 0]
     dma = pltpu.SemaphoreType.DMA
     vmem = pl.BlockSpec(memory_space=pltpu.VMEM)
     hbm = pl.BlockSpec(memory_space=pl.ANY)
     scratch = [
+        ((rows, cols), BF16),
         ((layers, cols, heads * head), BF16), ((layers, 4 * head, cols), BF16), ((layers, heads * head, cols), BF16),
         ((layers, cols, inner), BF16), ((layers, cols, inner), BF16), ((layers, inner, cols), BF16),
         ((seqs, head, seq_len), BF16), ((seqs, head, seq_len), BF16),
-        ((sums - 1, rows, cols), BF16), ((rows, cols), BF16), ((rows, inner), BF16),
+        ((sums, rows, cols), BF16), ((rows, cols), BF16), ((rows, inner), BF16),
         ((dec, LANES), jnp.int32), ((rows, LANES), F32), ((rows, LANES), F32),
         ((rows, heads * head), F32), ((rows, LANES), F32), ((rows, LANES), F32),
         ((heads, dec, LANES), F32), ((heads, dec, SEQS * head), F32), ((heads, chunk, LANES), BF16), ((heads, chunk, LANES), F32),
@@ -446,15 +458,15 @@
     ]
     for band in (dec, chunk):
         scratch += [((tp_size, band, width), BF16), ((sums, 4, band, width), BF16), ((sums, 3, band, width), BF16), ((sums, 3, band, width), BF16)]
-    semaphores = [(layers, 9), (layers, 2, CACHE_LOADS + 1)] + [(2 * sums, count) for count in (4, 4, 3, 3, 3, 3, 4, 4)]
+    semaphores = [(4,), (layers, 9), (layers, 2, CACHE_LOADS + 1)] + [(2 * sums, count) for count in (4, 4, 3, 3, 3, 3, 4, 4)]
     return pl.pallas_call(
         functools.partial(layer_kernel, tp_size // 2),
         out_shape=jax.ShapeDtypeStruct(x.shape, x.dtype),
-        in_specs=[vmem, pl.BlockSpec(memory_space=pltpu.SMEM), vmem, vmem, vmem] + [hbm] * 9,
-        out_specs=vmem,
+        in_specs=[hbm, pl.BlockSpec(memory_space=pltpu.SMEM), vmem, vmem] + [hbm] * 9,
+        out_specs=hbm,
         scratch_shapes=[pltpu.VMEM(shape, dtype) for shape, dtype in scratch] + [dma(shape) for shape in semaphores],
         compiler_params=pltpu.CompilerParams(collective_id=0, has_side_effects=True, vmem_limit_bytes=VMEM_LIMIT),
-    )(x, lengths, freq, attn_gain, mlp_gain, w_q, turned(w_k), turned(w_v), w_o, w_gate, w_up, w_down, k_cols, v_cols)
+    )(x, lengths, attn_gain, mlp_gain, w_q, turned(w_k), turned(w_v), w_o, w_gate, w_up, w_down, k_cols, v_cols)
 
 
 def solution(mesh):

time: 86.1 us -> 82.4 us (0.957)
  Pallas kernels: 83.1 us -> 80.1 us
    pallas_call x1, Pallas kernels: 83.1 us -> 80.1 us  [run_layers(): pl.pallas_call(functools.partial(layer_kernel, tp_size // 2), out_shape=j...]
where the time goes in v5:
time: 82.4 us; the launch traced here: 82.2 us
  Pallas kernels  80.1 us (97%)
  local copies, waits for them, and re-layouts  2.09 us (3%)
    pallas_call x1, Pallas kernels, run_layers(): pl.pallas_call(functools.partial(layer_kernel, tp_size // 2), out_shape=j...  80.1 us
    unnamed x1, local copies, waits for them, and re-layouts  2.09 us

profile of v5, /device:TPU:81, one launch (start us, length us, event | category | flops | bytes accessed | tf_op | source)
XLA Modules:
  0.0 82.2 jit_solution(3209130344541811399)
XLA Ops:
  0.0 80.1 %shard_map.127 = bf16[192,2048]{1,0:T(8,128)(2,1)} custom-call(bf16[192,2048]{1,0:T(8,128)(2,1)} %x_hbm.1, s32[65]{0:T(128)} %lens_ref.1, bf16[2,2048]{1,0:T(2,128)(2,1)} %again_ref.1, bf16[2,2048]{1,0:T(2,128)(2,1)} %mgain_ref.1, bf16[2,2048,256]{2,1,0:T(8,128)(2,1)} %wq_hbm.1, bf16[2,64,2048]{2,1,0:T(8,128)(2,1)} %bitcast.14, ...), custom_call_target="tpu_custom_call" | custom-call | tf_op jit(solution)/shard_map/pallas_call | solution.py:462
  80.1 2.1 %copy.17 = bf16[192,2048]{1,0:T(8,128)(2,1)} copy(bf16[192,2048]{1,0:T(8,128)(2,1)} %shard_map.127) | data formatting | bytes 1572864
